TPU v7x, 512 devices: a whole 4x8x8 slice. The times are simulated.
512 devices in a mesh: rx: 4 (over y_lo, core), ry: 4 (over x), tp: 32 (over z, y_hi).
Axes of the slice: x: 4, y: 8 (y_hi: 4, y_lo: 2; y = y_hi * 2 + y_lo), z: 8, core: 2. Of those that a mesh axis runs over, the one named last changes fastest.
Arguments:
- weights: float32 [4, 4, 2, 8192, 1024], P('rx', 'ry', None, 'tp'), may hold values from -6 to 6
- factors_rx: float32 [4, 4, 2, 8, 1024], P('rx', 'ry'), may hold values from -6 to 6
- factors_ry: float32 [4, 4, 2, 8, 1024], P('rx', 'ry'), may hold values from -6 to 6
Outputs:
- mixed_weights: float32 [4, 4, 2, 8192, 1024], P('rx', 'ry', None, 'tp')
- next_rx: float32 [4, 4, 2, 8, 1024], P('rx', 'ry')
- next_ry: float32 [4, 4, 2, 8, 1024], P('rx', 'ry')
All inputs are finite; a program needn't handle non-finite values.
Results may differ from a plain program's by a relative error of at most 0.00007.
Values sent between devices are 32-bit elements; how exact they have to be, the bound alone decides.
A program may use at most 64 MiB of HBM per device.

v0:
```python
import jax
import jax.numpy as jnp
from jax import lax
from jax.sharding import PartitionSpec as P

highest = lax.Precision.HIGHEST
mixing = 0.2


def shifted(value, axis, steps):
    count = lax.axis_size(axis)
    pairs = [(source, (source + steps) % count) for source in range(count)]
    return lax.ppermute(value, axis, pairs)


def extended(x, sides, width):
    edges = {}
    for axis, dim in sides:
        size, length = (lax.axis_size(axis), x.shape[dim])
        up = [(i, (i + 1) % size) for i in range(size)]
        last = lax.slice_in_dim(x, length - width, length, axis=dim)
        leading = lax.slice_in_dim(x, 0, width, axis=dim)
        edges[dim] = (
            lax.ppermute(last, axis, up),
            lax.ppermute(leading, axis, [(b, a) for a, b in up]),
        )
    done = []
    for _, dim in sides:
        low, high = edges[dim]
        around = [(width, width) if d in done else (0, 0) for d in range(x.ndim)]
        x = jnp.concatenate([jnp.pad(low, around), x, jnp.pad(high, around)], axis=dim)
        done.append(dim)
    return x


def sent_to_all(x, axis):
    size = lax.axis_size(axis)
    return lax.all_to_all(jnp.broadcast_to(x[None], (size, *x.shape)), axis, 0, 0, tiled=True)


def over_copies(x, axis):
    return sent_to_all(x, axis).sum(axis=0)


def in_blocks(x, dim, size):
    before, after = (x.shape[:dim], x.shape[dim + 1 :])
    return jnp.moveaxis(x.reshape(*before, size, -1, *after), dim, 0)


def sent_and_summed(x, axis, dim):
    size = lax.axis_size(axis)
    blocks = lax.all_to_all(in_blocks(x, dim, size), axis, 0, 0, tiled=True)
    return jnp.sum(blocks, axis=0)


def laid_out(blocks, dim):
    lengths = list(blocks.shape[1:])
    lengths[dim] *= blocks.shape[0]
    return jnp.moveaxis(blocks, 0, dim).reshape(lengths)


def collect(x, axis, dim):
    blocks = sent_to_all(x, axis)
    return laid_out(blocks, dim)


def select_edges(grid):
    return jnp.stack([grid[2, 1, 1], grid[0, 1, 0], grid[1, 2, 3], grid[1, 0, 2]], 0)


def per_device(weights, factors_rx, factors_ry):
    lower_rx = shifted(factors_rx, "rx", 1)
    lower_ry = shifted(factors_ry, "ry", 1)
    factor_set = jnp.stack([factors_rx[0, 0], lower_rx[0, 0], factors_ry[0, 0], lower_ry[0, 0]], 0)
    local_rows = weights[0, 0]
    projected = jnp.einsum("emrk,mdk->emrd", factor_set, local_rows, precision=highest)
    near_grid = extended(projected[None, None], (("rx", 0), ("ry", 1)), 1)
    differ = projected - select_edges(near_grid)
    gram_local = jnp.einsum("emrd,emsd->emrs", differ, differ, precision=highest)
    gram_total = over_copies(gram_local, "tp")
    lower_factor = jnp.linalg.cholesky(gram_total)
    normalised = lax.linalg.triangular_solve(lower_factor, differ, left_side=True, lower=True)
    back_terms = jnp.einsum("emrd,mdk->emrk", normalised, local_rows, precision=highest)
    shares = sent_and_summed(back_terms, "tp", 3)
    share_grid = extended(shares[None, None], (("rx", 0), ("ry", 1)), 1)
    updated = collect(shares + select_edges(share_grid), "tp", 3)
    correction = jnp.einsum("emrd,emrk->mdk", normalised, updated, precision=highest)
    mixed_weights = weights - mixing * correction[None, None]
    return (mixed_weights, updated[0][None, None], updated[2][None, None])


def solution(mesh):
    return jax.shard_map(
        per_device,
        mesh=mesh,
        in_specs=(
            P("rx", "ry", None, "tp", None),
            P("rx", "ry", None, None, None),
            P("rx", "ry", None, None, None),
        ),
        out_specs=(
            P("rx", "ry", None, "tp", None),
            P("rx", "ry", None, None, None),
            P("rx", "ry", None, None, None),
        ),
        check_vma=False,
    )
```

profile of v0, /device:TPU:1, one launch (start us, length us, event | category | flops | bytes accessed | tf_op | source)
XLA Modules:
  0.0 141.1 jit_solution(11370868545636197093)
XLA Ops:
  0.6 4.6 %collective-permute-start = (f32[1,1,2,8,1024]{4,3,2,1,0:T(8,128)}, f32[1,1,2,8,1024]{4,3,2,1,0:T(8,128)S(1)}, u32[]{:S(2)}, u32[]{:S(2)}) collective-permute-start(f32[1,1,2,8,1024]{4,3,2,1,0:T(8,128)} %param.4), channel_id=1, source_target_pairs={{0,128},{128,256},{256,384},{384,0},{1,129},{129,257},{257,385},{3... | collective-permute-start | bytes 196616 | tf_op jit(solution)/shard_map/ppermute | solution.py:13
  5.2 3.1 %collective-permute-start.1 = (f32[1,1,2,8,1024]{4,3,2,1,0:T(8,128)}, f32[1,1,2,8,1024]{4,3,2,1,0:T(8,128)S(1)}, u32[]{:S(2)}, u32[]{:S(2)}) collective-permute-start(f32[1,1,2,8,1024]{4,3,2,1,0:T(8,128)} %param.5), channel_id=1, source_target_pairs={{0,32},{32,64},{64,96},{96,0},{1,33},{33,65},{65,97},{97,1},{2,34}... | collective-permute-start | bytes 196616 | tf_op jit(solution)/shard_map/ppermute | solution.py:13
  8.3 2.0 %collective-permute-done = f32[1,1,2,8,1024]{4,3,2,1,0:T(8,128)S(1)} collective-permute-done((f32[1,1,2,8,1024]{4,3,2,1,0:T(8,128)}, f32[1,1,2,8,1024]{4,3,2,1,0:T(8,128)S(1)}, u32[]{:S(2)}, u32[]{:S(2)}) %collective-permute-start) | collective-permute-done | bytes 65568 | tf_op jit(solution)/shard_map/ppermute | solution.py:13
  10.3 1.3 collective-permute-done.1
  11.7 3.7 %fusion.7 = f32[4,2,8,256]{3,2,0,1:T(8,128)S(1)} fusion(f32[1,1,2,256,1024]{4,3,2,1,0:T(8,128)} %param.3, f32[1,2,8,1024]{3,2,0,1:T(8,128)S(1)} %bitcast.90, f32[1,2,8,1024]{3,2,0,1:T(8,128)} %bitcast.87, f32[1,2,8,1024]{3,2,0,1:T(8,128)S(1)} %bitcast.89, f32[1,2,8,1024]{3,2,0,1:T(8,128)} %bitcast.88), kind=kOutput, calls=%fused_computation.7 | convolution fusion | flops 201523200 | bytes 2424832 | tf_op jit(solution)/shard_map/emrk,mdk->emrd/dot_general | solution.py:76
  15.3 1.9 %collective-permute-start.5 = (f32[1,1,4,2,8,256]{5,4,3,2,1,0:T(8,128)S(1)}, f32[1,1,4,2,8,256]{5,4,3,2,1,0:T(8,128)S(1)}, u32[]{:S(2)}, u32[]{:S(2)}) collective-permute-start(f32[1,1,4,2,8,256]{5,4,3,2,1,0:T(8,128)S(1)} %bitcast.91), channel_id=1, source_target_pairs={{0,32},{32,64},{64,96},{96,0},{1,33},{33,65},{65,97},{97,1},{2,34}... | collective-permute-start | bytes 196616 | tf_op jit(solution)/shard_map/ppermute | solution.py:24
  17.3 4.6 %collective-permute-start.4 = (f32[1,1,4,2,8,256]{5,4,3,2,1,0:T(8,128)S(1)}, f32[1,1,4,2,8,256]{5,4,3,2,1,0:T(8,128)S(1)}, u32[]{:S(2)}, u32[]{:S(2)}) collective-permute-start(f32[1,1,4,2,8,256]{5,4,3,2,1,0:T(8,128)S(1)} %bitcast.92), channel_id=1, source_target_pairs={{32,0},{64,32},{96,64},{0,96},{33,1},{65,33},{97,65},{1,97},{34,2}... | collective-permute-start | bytes 196616 | tf_op jit(solution)/shard_map/ppermute | solution.py:25
  21.8 3.6 %collective-permute-start.3 = (f32[1,1,4,2,8,256]{5,4,3,2,1,0:T(8,128)S(1)}, f32[1,1,4,2,8,256]{5,4,3,2,1,0:T(8,128)S(1)}, u32[]{:S(2)}, u32[]{:S(2)}) collective-permute-start(f32[1,1,4,2,8,256]{5,4,3,2,1,0:T(8,128)S(1)} %bitcast.93), channel_id=1, source_target_pairs={{0,128},{128,256},{256,384},{384,0},{1,129},{129,257},{257,385},{3... | collective-permute-start | bytes 196616 | tf_op jit(solution)/shard_map/ppermute | solution.py:24
  25.5 6.1 %collective-permute-start.2 = (f32[1,1,4,2,8,256]{5,4,3,2,1,0:T(8,128)S(1)}, f32[1,1,4,2,8,256]{5,4,3,2,1,0:T(8,128)S(1)}, u32[]{:S(2)}, u32[]{:S(2)}) collective-permute-start(f32[1,1,4,2,8,256]{5,4,3,2,1,0:T(8,128)S(1)} %bitcast.94), channel_id=1, source_target_pairs={{128,0},{256,128},{384,256},{0,384},{129,1},{257,129},{385,257},{1... | collective-permute-start | bytes 196616 | tf_op jit(solution)/shard_map/ppermute | solution.py:25
  31.6 1.9 %collective-permute-done.2 = f32[1,1,4,2,8,256]{5,4,3,2,1,0:T(8,128)S(1)} collective-permute-done((f32[1,1,4,2,8,256]{5,4,3,2,1,0:T(8,128)S(1)}, f32[1,1,4,2,8,256]{5,4,3,2,1,0:T(8,128)S(1)}, u32[]{:S(2)}, u32[]{:S(2)}) %collective-permute-start.2) | collective-permute-done | bytes 65568 | tf_op jit(solution)/shard_map/ppermute | solution.py:25
  35.0 12.6 %all-to-all-start = ((f32[32,1,512]{2,1,0:T(1,128)}), f32[32,1,512]{2,1,0:T(1,128)S(1)}, u32[]{:S(2)}, u32[]{:S(2)}) async-start(f32[32,1,512]{2,1,0:T(1,128)} %reshape.67), calls=%async_computation | async-start | bytes 131072 | tf_op jit(solution)/shard_map/all_to_all | solution.py:38
  47.6 11.1 %all-to-all-done = f32[32,1,512]{2,1,0:T(1,128)S(1)} async-done(((f32[32,1,512]{2,1,0:T(1,128)}), f32[32,1,512]{2,1,0:T(1,128)S(1)}, u32[]{:S(2)}, u32[]{:S(2)}) %all-to-all-start) | async-done | bytes 65568 | tf_op jit(solution)/shard_map/all_to_all | solution.py:38
  60.8 5.8 %custom-call.7 = f32[4,2,8,8]{3,2,1,0:T(8,128)S(1)} custom-call(f32[4,2,8,8]{3,2,1,0:T(8,128)S(1)} %fusion.23), custom_call_target="Cholesky" | custom-call | tf_op jit(solution)/shard_map/jit(cholesky)/cholesky | solution.py:81
  66.9 5.0 %custom-call.8 = f32[4,2,1,8,8]{3,4,2,1,0:T(8,128)S(1)} custom-call(f32[4,2,1,8,8]{4,3,2,1,0:T(8,128)S(1)} %select_bitcast_fusion), custom_call_target="InvertDiagBlocksLowerTriangular" | custom-call | tf_op jit(solution)/shard_map/triangular_solve | solution.py:82
  73.9 1.6 %copy.106 = f32[4,2,8,32,32]{4,2,0,1,3:T(8,128)} copy(f32[4,2,8,32,32]{4,3,2,0,1:T(8,128)S(1)} %reshape.63) | data formatting | bytes 524288 | tf_op jit(solution)/shard_map/reshape | solution.py:47
  75.5 1.7 %reshape.69 = f32[32,1,2048]{2,1,0:T(1,128)S(1)} reshape(f32[32,2,4,8,32]{4,3,2,1,0:T(8,128)} %bitcast.86) | data formatting | bytes 524288
  77.2 14.7 %all_to_all.15 = f32[32,1,2048]{2,1,0:T(1,128)S(1)} all-to-all(f32[32,1,2048]{2,1,0:T(1,128)S(1)} %reshape.69), channel_id=1, replica_groups=mesh['rx'=4,'ry'=4,'tp'=32] {'tp'}, dimensions={0} | all-to-all | bytes 524288 | tf_op jit(solution)/shard_map/all_to_all | solution.py:52
  93.6 1.9 %collective-permute-start.9 = (f32[1,1,4,2,8,32]{5,4,3,2,1,0:T(8,128)S(1)}, f32[1,1,4,2,8,32]{5,4,3,2,1,0:T(8,128)S(1)}, u32[]{:S(2)}, u32[]{:S(2)}) collective-permute-start(f32[1,1,4,2,8,32]{5,4,3,2,1,0:T(8,128)S(1)} %bitcast.95), channel_id=1, source_target_pairs={{0,32},{32,64},{64,96},{96,0},{1,33},{33,65},{65,97},{97,1},{2,34}... | collective-permute-start | bytes 24584 | tf_op jit(solution)/shard_map/ppermute | solution.py:24
  95.5 4.6 %collective-permute-start.8 = (f32[1,1,4,2,8,32]{5,4,3,2,1,0:T(8,128)S(1)}, f32[1,1,4,2,8,32]{5,4,3,2,1,0:T(8,128)S(1)}, u32[]{:S(2)}, u32[]{:S(2)}) collective-permute-start(f32[1,1,4,2,8,32]{5,4,3,2,1,0:T(8,128)S(1)} %bitcast.96), channel_id=1, source_target_pairs={{32,0},{64,32},{96,64},{0,96},{33,1},{65,33},{97,65},{1,97},{34,2}... | collective-permute-start | bytes 24584 | tf_op jit(solution)/shard_map/ppermute | solution.py:25
  100.1 7.3 %collective-permute-start.7 = (f32[1,1,4,2,8,32]{5,4,3,2,1,0:T(8,128)S(1)}, f32[1,1,4,2,8,32]{5,4,3,2,1,0:T(8,128)S(1)}, u32[]{:S(2)}, u32[]{:S(2)}) collective-permute-start(f32[1,1,4,2,8,32]{5,4,3,2,1,0:T(8,128)S(1)} %bitcast.97), channel_id=1, source_target_pairs={{0,128},{128,256},{256,384},{384,0},{1,129},{129,257},{257,385},{3... | collective-permute-start | bytes 24584 | tf_op jit(solution)/shard_map/ppermute | solution.py:24
  107.4 1.9 %collective-permute-start.6 = (f32[1,1,4,2,8,32]{5,4,3,2,1,0:T(8,128)S(1)}, f32[1,1,4,2,8,32]{5,4,3,2,1,0:T(8,128)S(1)}, u32[]{:S(2)}, u32[]{:S(2)}) collective-permute-start(f32[1,1,4,2,8,32]{5,4,3,2,1,0:T(8,128)S(1)} %bitcast.98), channel_id=1, source_target_pairs={{128,0},{256,128},{384,256},{0,384},{129,1},{257,129},{385,257},{1... | collective-permute-start | bytes 24584 | tf_op jit(solution)/shard_map/ppermute | solution.py:25
  109.4 3.2 %collective-permute-done.6 = f32[1,1,4,2,8,32]{5,4,3,2,1,0:T(8,128)S(1)} collective-permute-done((f32[1,1,4,2,8,32]{5,4,3,2,1,0:T(8,128)S(1)}, f32[1,1,4,2,8,32]{5,4,3,2,1,0:T(8,128)S(1)}, u32[]{:S(2)}, u32[]{:S(2)}) %collective-permute-start.6) | collective-permute-done | bytes 8224 | tf_op jit(solution)/shard_map/ppermute | solution.py:25
  113.2 17.3 %all_to_all.16 = f32[32,1,2048]{2,1,0:T(1,128)S(1)} all-to-all(f32[32,1,2048]{2,1,0:T(1,128)S(1)} %reshape.71), channel_id=1, replica_groups=mesh['rx'=4,'ry'=4,'tp'=32] {'tp'}, dimensions={0} | all-to-all | bytes 524288 | tf_op jit(solution)/shard_map/all_to_all | solution.py:38
  137.8 3.2 %bitcast_subtract_fusion = f32[1,1,2,256,1024]{4,3,2,1,0:T(8,128)} fusion(f32[1,1,2,256,1024]{4,3,2,1,0:T(8,128)S(1)} %copy-done, f32[4,2,8,256]{3,2,1,0:T(8,128)S(1)} %fusion.18, f32[4,2,8,1024]{3,2,1,0:T(8,128)S(1)} %reshape.64), kind=kOutput, calls=%fused_computation | convolution fusion | flops 202375168 | bytes 4521984 | tf_op jit(solution)/shard_map/emrd,emrk->mdk/dot_general | solution.py:87
  (51 shorter events, 15.3 us)
Async XLA Ops:
  0.6 9.7 %collective-permute-start = (f32[1,1,2,8,1024]{4,3,2,1,0:T(8,128)}, f32[1,1,2,8,1024]{4,3,2,1,0:T(8,128)S(1)}, u32[]{:S(2)}, u32[]{:S(2)}) collective-permute-start(f32[1,1,2,8,1024]{4,3,2,1,0:T(8,128)} %param.4), channel_id=1, source_target_pairs={{0,128},{128,256},{256,384},{384,0},{1,129},{129,257},{257,385},{3... | collective-permute-start | bytes 196616 | tf_op jit(solution)/shard_map/ppermute | solution.py:13
  5.2 6.4 %collective-permute-start.1 = (f32[1,1,2,8,1024]{4,3,2,1,0:T(8,128)}, f32[1,1,2,8,1024]{4,3,2,1,0:T(8,128)S(1)}, u32[]{:S(2)}, u32[]{:S(2)}) collective-permute-start(f32[1,1,2,8,1024]{4,3,2,1,0:T(8,128)} %param.5), channel_id=1, source_target_pairs={{0,32},{32,64},{64,96},{96,0},{1,33},{33,65},{65,97},{97,1},{2,34}... | collective-permute-start | bytes 196616 | tf_op jit(solution)/shard_map/ppermute | solution.py:13
  15.3 16.2 %collective-permute-start.5 = (f32[1,1,4,2,8,256]{5,4,3,2,1,0:T(8,128)S(1)}, f32[1,1,4,2,8,256]{5,4,3,2,1,0:T(8,128)S(1)}, u32[]{:S(2)}, u32[]{:S(2)}) collective-permute-start(f32[1,1,4,2,8,256]{5,4,3,2,1,0:T(8,128)S(1)} %bitcast.91), channel_id=1, source_target_pairs={{0,32},{32,64},{64,96},{96,0},{1,33},{33,65},{65,97},{97,1},{2,34}... | collective-permute-start | bytes 196616 | tf_op jit(solution)/shard_map/ppermute | solution.py:24
  17.3 14.3 %collective-permute-start.4 = (f32[1,1,4,2,8,256]{5,4,3,2,1,0:T(8,128)S(1)}, f32[1,1,4,2,8,256]{5,4,3,2,1,0:T(8,128)S(1)}, u32[]{:S(2)}, u32[]{:S(2)}) collective-permute-start(f32[1,1,4,2,8,256]{5,4,3,2,1,0:T(8,128)S(1)} %bitcast.92), channel_id=1, source_target_pairs={{32,0},{64,32},{96,64},{0,96},{33,1},{65,33},{97,65},{1,97},{34,2}... | collective-permute-start | bytes 196616 | tf_op jit(solution)/shard_map/ppermute | solution.py:25
  21.8 9.8 %collective-permute-start.3 = (f32[1,1,4,2,8,256]{5,4,3,2,1,0:T(8,128)S(1)}, f32[1,1,4,2,8,256]{5,4,3,2,1,0:T(8,128)S(1)}, u32[]{:S(2)}, u32[]{:S(2)}) collective-permute-start(f32[1,1,4,2,8,256]{5,4,3,2,1,0:T(8,128)S(1)} %bitcast.93), channel_id=1, source_target_pairs={{0,128},{128,256},{256,384},{384,0},{1,129},{129,257},{257,385},{3... | collective-permute-start | bytes 196616 | tf_op jit(solution)/shard_map/ppermute | solution.py:24
  25.5 8.0 %collective-permute-start.2 = (f32[1,1,4,2,8,256]{5,4,3,2,1,0:T(8,128)S(1)}, f32[1,1,4,2,8,256]{5,4,3,2,1,0:T(8,128)S(1)}, u32[]{:S(2)}, u32[]{:S(2)}) collective-permute-start(f32[1,1,4,2,8,256]{5,4,3,2,1,0:T(8,128)S(1)} %bitcast.94), channel_id=1, source_target_pairs={{128,0},{256,128},{384,256},{0,384},{129,1},{257,129},{385,257},{1... | collective-permute-start | bytes 196616 | tf_op jit(solution)/shard_map/ppermute | solution.py:25
  33.8 38.4 %copy-start = (f32[1,1,2,256,1024]{4,3,2,1,0:T(8,128)S(1)}, f32[1,1,2,256,1024]{4,3,2,1,0:T(8,128)}, u32[]{:S(2)}) copy-start(f32[1,1,2,256,1024]{4,3,2,1,0:T(8,128)} %param.3) | copy-start | bytes 6291460
  35.0 23.7 %all-to-all-start = ((f32[32,1,512]{2,1,0:T(1,128)}), f32[32,1,512]{2,1,0:T(1,128)S(1)}, u32[]{:S(2)}, u32[]{:S(2)}) async-start(f32[32,1,512]{2,1,0:T(1,128)} %reshape.67), calls=%async_computation | async-start | bytes 131072 | tf_op jit(solution)/shard_map/all_to_all | solution.py:38
  93.6 15.7 %collective-permute-start.9 = (f32[1,1,4,2,8,32]{5,4,3,2,1,0:T(8,128)S(1)}, f32[1,1,4,2,8,32]{5,4,3,2,1,0:T(8,128)S(1)}, u32[]{:S(2)}, u32[]{:S(2)}) collective-permute-start(f32[1,1,4,2,8,32]{5,4,3,2,1,0:T(8,128)S(1)} %bitcast.95), channel_id=1, source_target_pairs={{0,32},{32,64},{64,96},{96,0},{1,33},{33,65},{65,97},{97,1},{2,34}... | collective-permute-start | bytes 24584 | tf_op jit(solution)/shard_map/ppermute | solution.py:24
  95.5 13.8 %collective-permute-start.8 = (f32[1,1,4,2,8,32]{5,4,3,2,1,0:T(8,128)S(1)}, f32[1,1,4,2,8,32]{5,4,3,2,1,0:T(8,128)S(1)}, u32[]{:S(2)}, u32[]{:S(2)}) collective-permute-start(f32[1,1,4,2,8,32]{5,4,3,2,1,0:T(8,128)S(1)} %bitcast.96), channel_id=1, source_target_pairs={{32,0},{64,32},{96,64},{0,96},{33,1},{65,33},{97,65},{1,97},{34,2}... | collective-permute-start | bytes 24584 | tf_op jit(solution)/shard_map/ppermute | solution.py:25
  100.1 9.3 %collective-permute-start.7 = (f32[1,1,4,2,8,32]{5,4,3,2,1,0:T(8,128)S(1)}, f32[1,1,4,2,8,32]{5,4,3,2,1,0:T(8,128)S(1)}, u32[]{:S(2)}, u32[]{:S(2)}) collective-permute-start(f32[1,1,4,2,8,32]{5,4,3,2,1,0:T(8,128)S(1)} %bitcast.97), channel_id=1, source_target_pairs={{0,128},{128,256},{256,384},{384,0},{1,129},{129,257},{257,385},{3... | collective-permute-start | bytes 24584 | tf_op jit(solution)/shard_map/ppermute | solution.py:24
  107.4 5.2 %collective-permute-start.6 = (f32[1,1,4,2,8,32]{5,4,3,2,1,0:T(8,128)S(1)}, f32[1,1,4,2,8,32]{5,4,3,2,1,0:T(8,128)S(1)}, u32[]{:S(2)}, u32[]{:S(2)}) collective-permute-start(f32[1,1,4,2,8,32]{5,4,3,2,1,0:T(8,128)S(1)} %bitcast.98), channel_id=1, source_target_pairs={{128,0},{256,128},{384,256},{0,384},{129,1},{257,129},{385,257},{1... | collective-permute-start | bytes 24584 | tf_op jit(solution)/shard_map/ppermute | solution.py:25
where the time goes:
time: 142 us; the launch traced here: 141 us
  starting transfers between devices  52.2 us (37%)
  blocking collectives  32 us (23%)
  waiting for transfers between devices  19.5 us (14%)
  other arithmetic  14.7 us (10%)
  local copies, waits for them, and re-layouts  12.9 us (9%)
  matrix products  8.68 us (6%)
    all_to_all x1, blocking collectives, sent_to_all(): lax.all_to_all(jnp.broadcast_to(x[None], (size, *x.shape)), axis, 0, 0, t...  17.3 us
    ppermute x4, starting transfers between devices, extended(): lax.ppermute(leading, axis, [(b, a) for a, b in up])  17.2 us
    ppermute x4, starting transfers between devices, extended(): lax.ppermute(last, axis, up)  14.7 us
    all_to_all x1, blocking collectives, sent_and_summed(): blocks = lax.all_to_all(in_blocks(x, dim, size), axis, 0, 0, tiled=True)  14.7 us
    all_to_all x1, starting transfers between devices, sent_to_all(): lax.all_to_all(jnp.broadcast_to(x[None], (size, *x.shape)), axis, 0, 0, t...  12.6 us
    all_to_all x1, waiting for transfers between devices, sent_to_all(): lax.all_to_all(jnp.broadcast_to(x[None], (size, *x.shape)), axis, 0, 0, t...  11.1 us
    ppermute x2, starting transfers between devices, shifted(): return lax.ppermute(value, axis, pairs)  7.7 us
    another operation x4, other arithmetic, per_device(): lower_factor = jnp.linalg.cholesky(gram_total)  6.07 us
  transfers between devices with their start and end apart: 11, of which 5 were waited for; matrix products, arithmetic and copies ran while one was open for 0% of the time, Pallas kernels for 0%

commit v1 on v0

v1 whole, which is shorter than its diff:
```python
import jax
import jax.numpy as jnp
from jax import lax
from jax.experimental import pallas as pl
from jax.experimental.pallas import tpu as pltpu
from jax.sharding import PartitionSpec as P

MESH = pl.DeviceIdType.MESH
F32 = jnp.float32
BF16 = jnp.bfloat16
NZ, NY = 8, 4
FAR_FIRST = (4, 3, 5, 2, 6, 1, 7)
NT = (((1,), (1,)), ((), ()))
NN = (((1,), (0,)), ((), ()))


def split3(x):
    hi = x.astype(BF16)
    rest = x - hi.astype(F32)
    mid = rest.astype(BF16)
    low = (rest - mid.astype(F32)).astype(BF16)
    return hi, mid, low


def dot6(x, wh, wm, wl, dims):
    rows = x.shape[0]
    hi, mid, low = split3(x)
    a = lax.dot_general(jnp.concatenate([hi, mid, low], 0), wh, dims, preferred_element_type=F32)
    b = lax.dot_general(jnp.concatenate([hi, mid], 0), wm, dims, preferred_element_type=F32)
    c = lax.dot_general(hi, wl, dims, preferred_element_type=F32)
    small = (c + b[rows:]) + a[2 * rows :]
    return a[:rows] + ((a[rows : 2 * rows] + b[:rows]) + small)


def lanes_of(x):
    return x.reshape(-1, x.shape[-1])


def gossip(
    w_hbm, fx_hbm, fy_hbm, r_out, h_out,
    q, wv, wh, wm, wl, own, nb, p, c0, c1, r0, r1, g1, g2, s0, s1, q0o, q0n, q1o, q1n, f0, f1,
    local_sem, fac_s, fac_r, own_s, own_r, a0_s, a0_r, a1_s, a1_r, g1_s, g1_r, g2_s, g2_r,
    b0_s, b0_r, b0n_s, b0n_r, b1_s, b1_r, b1n_s, b1n_r, d0_s, d0_r, d1_s, d1_r, e0_s, e0_r, e1_s, e1_r,
):
    a, b, t = lax.axis_index("rx"), lax.axis_index("ry"), lax.axis_index("tp")
    z, y = t // NY, t % NY
    ap, am, bp, bm = (a + 1) % 4, (a + 3) % 4, (b + 1) % 4, (b + 3) % 4
    pa, pb = 2 * (a % 2), 2 * (b % 2)

    def owner(slot):
        par = pa if slot % 2 == 0 else pb
        return (slot + par) % 4

    par_me = jnp.where(y % 2 == 0, pa, pb)
    mine = (y + par_me) % 4
    near = [(am, b), (a, bm), (ap, b), (a, bp)]
    is_x = y % 2 == 0
    upper = mine >= 2
    my_a = jnp.where(is_x, jnp.where(upper, ap, am), a)
    my_b = jnp.where(is_x, b, jnp.where(upper, bp, bm))

    def at(ra, rb, zz, yy):
        return (ra, rb, zz * NY + yy)

    def zk(k):
        return (z + k) % NZ

    def yk(k):
        return (y + k) % NY

    def send(src, dst, ssem, rsem, dev):
        copy = pltpu.make_async_remote_copy(
            src_ref=src, dst_ref=dst, send_sem=ssem, recv_sem=rsem, device_id=dev, device_id_type=MESH
        )
        copy.start()
        return copy

    def landed(dst, rsem):
        pltpu.make_async_remote_copy(
            src_ref=dst, dst_ref=dst, send_sem=rsem, recv_sem=rsem, device_id=near_dev[0], device_id_type=MESH
        ).wait_recv()

    near_dev = [(ra, rb, t) for ra, rb in near]
    pending = []

    loads = [
        pltpu.make_async_copy(fx_hbm, q.at[2], local_sem.at[0]),
        pltpu.make_async_copy(fy_hbm, q.at[3], local_sem.at[1]),
        pltpu.make_async_copy(w_hbm.at[0], wv.at[0], local_sem.at[2]),
        pltpu.make_async_copy(w_hbm.at[1], wv.at[1], local_sem.at[3]),
    ]
    for load in loads:
        load.start()

    barrier = pltpu.get_barrier_semaphore()

    def greet(dev):
        pl.semaphore_signal(barrier, inc=1, device_id=dev, device_id_type=MESH)

    for dev in near_dev:
        greet(dev)
    for k in range(1, NZ):
        greet(at(a, b, zk(k), y))
    for k in range(1, NY):
        greet(at(a, b, z, yk(k)))
    for k in range(NY):
        greet(at(my_a, my_b, z, yk(k)))
    for k in range(NZ):
        greet(at(my_a, my_b, zk(k), y))

    for load in loads:
        load.wait()
    for m in range(2):
        hi, mid, low = split3(wv[m])
        wh[m], wm[m], wl[m] = hi, mid, low

    def project(first):
        for m in range(2):
            x = jnp.concatenate([q[first, m], q[first + 1, m]], 0)
            res = dot6(x, wh[m], wm[m], wl[m], NT)
            own[first, m] = res[:8]
            own[first + 1, m] = res[8:]

    project(2)
    pl.semaphore_wait(barrier, 4 + 7 + 3 + NY + NZ)

    pending.append(send(q.at[2], q.at[0], fac_s.at[0], fac_r.at[0], near_dev[2]))
    pending.append(send(q.at[3], q.at[1], fac_s.at[1], fac_r.at[1], near_dev[3]))
    for s in (2, 3):
        pending.append(send(own.at[s], nb.at[s ^ 2], own_s.at[s], own_r.at[s ^ 2], near_dev[s]))
    for s in (0, 1):
        landed(q.at[s], fac_r.at[s])
    project(0)
    for s in (0, 1):
        pending.append(send(own.at[s], nb.at[s ^ 2], own_s.at[s], own_r.at[s ^ 2], near_dev[s]))

    def differ(first):
        for s in (first, first + 1):
            landed(nb.at[s], own_r.at[s])
            for m in range(2):
                p[m, s] = own[s, m] - nb[s, m]

    def back(first):
        half = first // 2
        for m in range(2):
            x = lanes_of(p[m, pl.ds(first, 2)])
            res = dot6(x, wh[m], wm[m], wl[m], NN)
            for i in range(2):
                for j in range(NZ):
                    tile = res[8 * i : 8 * i + 8, 128 * j : 128 * j + 128]
                    if m == 0:
                        c0[j, first + i] = tile
                    else:
                        c1[first + i, j] = tile
            if m == 0:
                for k in FAR_FIRST:
                    part = pl.ds(first, 2)
                    pending.append(
                        send(
                            c0.at[zk(k), part], r0.at[k - 1, part],
                            a0_s.at[half, k - 1], a0_r.at[half, k - 1], at(a, b, zk(k), y),
                        )
                    )
            else:
                for s in (first, first + 1):
                    yy = owner(s)
                    k = (yy - y + NY) % NY

                    @pl.when(k != 0)
                    def _():
                        send(c1.at[s], r1.at[(k + 3) % 4], a1_s.at[s], a1_r.at[(k + 3) % 4], at(a, b, z, yy))

    differ(0)
    back(0)
    differ(2)

    rows = p[...].reshape(64, 256)
    gram = lax.dot_general(
        rows, jnp.concatenate([rows, rows], 0), NT, precision=lax.Precision.HIGHEST, preferred_element_type=F32
    )
    lane = lax.broadcasted_iota(jnp.int32, (8, 128), 1)
    block = (lane // 8) % 8
    tile = jnp.zeros((8, 128), F32)
    for i in range(8):
        tile = tile + jnp.where(block == i, gram[8 * i : 8 * i + 8], 0.0)
    g1[y] = tile
    for k in (2, 1, 3):
        pending.append(send(g1.at[y], g1.at[y], g1_s.at[k - 1], g1_r.at[k - 1], at(a, b, z, yk(k))))

    back(2)

    for k in range(1, NY):
        landed(g1.at[(y + NY - k) % NY], g1_r.at[k - 1])
    g2[z] = (g1[0] + g1[1]) + (g1[2] + g1[3])
    for k in FAR_FIRST:
        pending.append(send(g2.at[z], g2.at[z], g2_s.at[k - 1], g2_r.at[k - 1], at(a, b, zk(k), y)))

    for k in range(1, NZ):
        for half in range(2):
            landed(r0.at[k - 1, pl.ds(2 * half, 2)], a0_r.at[half, k - 1])
    total = c0[z]
    for k in range(1, NZ):
        total = total + r0[k - 1]
    s0[...] = total
    for s in range(4):
        yy = owner(s)
        k = (yy - y + NY) % NY
        pending.append(send(s0.at[s], q0n.at[y], b0n_s.at[s], b0n_r.at[y], at(*near[s], z, yy)))

        @pl.when(k != 0)
        def _():
            send(s0.at[s], q0o.at[(k + 3) % 4], b0_s.at[s], b0_r.at[(k + 3) % 4], at(a, b, z, yy))

    for k in range(1, NY):
        landed(r1.at[k - 1], a1_r.at[k - 1])
    s1[...] = (c1[mine] + r1[0]) + (r1[1] + r1[2])
    for k in FAR_FIRST:
        zz = zk(k)
        pending.append(send(s1.at[zz], q1n.at[z], b1n_s.at[k], b1n_r.at[z], at(my_a, my_b, zz, y)))
        pending.append(send(s1.at[zz], q1o.at[k - 1], b1_s.at[k - 1], b1_r.at[k - 1], at(a, b, zz, y)))
    pending.append(send(s1.at[z], q1n.at[z], b1n_s.at[0], b1n_r.at[z], at(my_a, my_b, z, y)))

    for k in range(NY):
        landed(q0n.at[k], b0n_r.at[k])
    for k in range(1, NY):
        landed(q0o.at[k - 1], b0_r.at[k - 1])
    total = (s0[mine] + q0o[0]) + (q0o[1] + q0o[2])
    f0[z, mine] = total + ((q0n[0] + q0n[1]) + (q0n[2] + q0n[3]))
    for k in (2, 1, 3):
        pending.append(
            send(f0.at[z, mine], f0.at[z, mine], d0_s.at[k - 1], d0_r.at[k - 1], at(a, b, z, yk(k)))
        )

    for k in range(NZ):
        landed(q1n.at[k], b1n_r.at[k])
    for k in range(1, NZ):
        landed(q1o.at[k - 1], b1_r.at[k - 1])
    total = s1[z]
    for k in range(1, NZ):
        total = total + q1o[k - 1]
    other = q1n[0]
    for k in range(1, NZ):
        other = other + q1n[k]
    f1[mine, z] = total + other
    for k in FAR_FIRST:
        pending.append(
            send(f1.at[mine, z], f1.at[mine, z], d1_s.at[k - 1], d1_r.at[k - 1], at(a, b, zk(k), y))
        )

    def slot_of(yy):
        return (yy + jnp.where(yy % 2 == 0, pa, pb)) % 4

    for k in range(1, NY):
        landed(f0.at[z, slot_of((y + NY - k) % NY)], d0_r.at[k - 1])
    for k in FAR_FIRST:
        pending.append(send(f0.at[z], f0.at[z], e0_s.at[k - 1], e0_r.at[k - 1], at(a, b, zk(k), y)))

    for k in range(1, NZ):
        landed(f1.at[mine, (z + NZ - k) % NZ], d1_r.at[k - 1])
    for k in (2, 1, 3):
        pending.append(send(f1.at[mine], f1.at[mine], e1_s.at[k - 1], e1_r.at[k - 1], at(a, b, z, yk(k))))

    for k in range(1, NZ):
        landed(g2.at[(z + NZ - k) % NZ], g2_r.at[k - 1])
    tile = ((g2[0] + g2[1]) + (g2[2] + g2[3])) + ((g2[4] + g2[5]) + (g2[6] + g2[7]))
    row = lax.broadcasted_iota(jnp.int32, (8, 128), 0)
    cols = [tile] + [pltpu.roll(tile, 128 - j, 1) for j in range(1, 8)]
    lower, inverse_diag = [], []
    for k in range(8):
        pivot = jnp.broadcast_to(cols[k][k : k + 1], (8, 128))
        inv = 1.0 / jnp.sqrt(pivot)
        col = cols[k] * inv
        lower.append(jnp.where(row > k, col, 0.0))
        inverse_diag.append(inv)
        for j in range(k + 1, 8):
            cols[j] = cols[j] - col * jnp.broadcast_to(col[j : j + 1], (8, 128))
    inv_cols = [jnp.where(row == j, 1.0, 0.0).astype(F32) for j in range(8)]
    for k in range(8):
        for j in range(k + 1):
            cur = inv_cols[j]
            pivot_row = jnp.broadcast_to(cur[k : k + 1], (8, 128)) * inverse_diag[k]
            cur = cur - lower[k] * pivot_row
            inv_cols[j] = jnp.where(row == k, pivot_row, cur)

    def solve(i, x):
        total = inv_cols[0][:, 8 * i : 8 * i + 1] * x[0:1]
        for j in range(1, 8):
            total = total + inv_cols[j][:, 8 * i : 8 * i + 1] * x[j : j + 1]
        return total

    for m in range(2):
        for s in range(4):
            h_out[m, s] = solve(4 * m + s, p[m, s])

    for k in range(1, NZ):
        landed(f0.at[(z + NZ - k) % NZ], e0_r.at[k - 1])
    for s in range(4):
        r_out[0, s] = solve(s, jnp.concatenate([f0[j, s] for j in range(NZ)], 1))
    for k in range(1, NY):
        landed(f1.at[slot_of((y + NY - k) % NY)], e1_r.at[k - 1])
    for s in range(4):
        r_out[1, s] = solve(4 + s, jnp.concatenate([f1[s, j] for j in range(NZ)], 1))

    for copy in pending:
        copy.wait_send()
    for s in range(4):

        @pl.when(owner(s) != y)
        def _():
            pltpu.make_async_remote_copy(
                src_ref=c1.at[s], dst_ref=c1.at[s], send_sem=a1_s.at[s], recv_sem=a1_s.at[s],
                device_id=near_dev[0], device_id_type=MESH,
            ).wait_send()
            pltpu.make_async_remote_copy(
                src_ref=s0.at[s], dst_ref=s0.at[s], send_sem=b0_s.at[s], recv_sem=b0_s.at[s],
                device_id=near_dev[0], device_id_type=MESH,
            ).wait_send()


CHUNKS = 4


def mix(w_hbm, h_ref, r_ref, out_hbm, nx_hbm, ny_hbm, wv, ov, in_sem, out_sem, small_sem):
    rows = 512 // CHUNKS

    def part(ref, i):
        return ref.at[i * rows // 256, pl.ds((i * rows) % 256, rows)]

    loads = [pltpu.make_async_copy(part(w_hbm, i), wv.at[i], in_sem.at[i]) for i in range(CHUNKS)]
    for load in loads:
        load.start()
    smalls = []
    for m in range(2):
        smalls.append(pltpu.make_async_copy(r_ref.at[m, 2], nx_hbm.at[m], small_sem.at[m]))
        smalls.append(pltpu.make_async_copy(r_ref.at[m, 3], ny_hbm.at[m], small_sem.at[2 + m]))
    for small in smalls:
        small.start()
    stores = []
    for m in range(2):
        h = h_ref[m].reshape(32, 256)
        r = r_ref[m].reshape(32, 1024)
        hh, hl, _ = split3(h)
        rh, rl, _ = split3(r)
        left = jnp.concatenate([hh, hh, hl], 0)
        right = jnp.concatenate([rh, rl, rh], 0)
        for i in range(m * CHUNKS // 2, (m + 1) * CHUNKS // 2):
            start = (i * rows) % 256
            loads[i].wait()
            term = lax.dot_general(
                left[:, start : start + rows], right, (((0,), (0,)), ((), ())), preferred_element_type=F32
            )
            ov[i] = wv[i] - 0.2 * term
            store = pltpu.make_async_copy(ov.at[i], part(out_hbm, i), out_sem.at[i])
            store.start()
            stores.append(store)
    for copy in smalls + stores:
        copy.wait()


def per_device(weights, factors_rx, factors_ry):
    w = weights.reshape(2, 256, 1024)
    vm = pltpu.VMEM
    dma = pltpu.SemaphoreType.DMA
    anyspec = pl.BlockSpec(memory_space=pl.ANY)
    vmem = pl.BlockSpec(memory_space=pltpu.VMEM)
    tile = (8, 128)
    r, h = pl.pallas_call(
        gossip,
        out_shape=(
            jax.ShapeDtypeStruct((2, 4, 8, 1024), F32),
            jax.ShapeDtypeStruct((2, 4, 8, 256), F32),
        ),
        in_specs=[anyspec] * 3,
        out_specs=(vmem, vmem),
        scratch_shapes=[
            vm((4, 2, 8, 1024), F32),
            vm((2, 256, 1024), F32),
            vm((2, 256, 1024), BF16),
            vm((2, 256, 1024), BF16),
            vm((2, 256, 1024), BF16),
            vm((4, 2, 8, 256), F32),
            vm((4, 2, 8, 256), F32),
            vm((2, 4, 8, 256), F32),
            vm((NZ, 4, *tile), F32),
            vm((4, NZ, *tile), F32),
            vm((NZ - 1, 4, *tile), F32),
            vm((NY - 1, NZ, *tile), F32),
            vm((NY, *tile), F32),
            vm((NZ, *tile), F32),
            vm((4, *tile), F32),
            vm((NZ, *tile), F32),
            vm((NY - 1, *tile), F32),
            vm((NY, *tile), F32),
            vm((NZ - 1, *tile), F32),
            vm((NZ, *tile), F32),
            vm((NZ, 4, *tile), F32),
            vm((4, NZ, *tile), F32),
            dma((4,)),
            dma((2,)), dma((2,)),
            dma((4,)), dma((4,)),
            dma((2, NZ - 1)), dma((2, NZ - 1)),
            dma((4,)), dma((NY - 1,)),
            dma((NY - 1,)), dma((NY - 1,)),
            dma((NZ - 1,)), dma((NZ - 1,)),
            dma((4,)), dma((NY - 1,)),
            dma((4,)), dma((NY,)),
            dma((NZ - 1,)), dma((NZ - 1,)),
            dma((NZ,)), dma((NZ,)),
            dma((NY - 1,)), dma((NY - 1,)),
            dma((NZ - 1,)), dma((NZ - 1,)),
            dma((NZ - 1,)), dma((NZ - 1,)),
            dma((NY - 1,)), dma((NY - 1,)),
        ],
        compiler_params=pltpu.CompilerParams(
            collective_id=0, has_side_effects=True, vmem_limit_bytes=24 * 1024 * 1024
        ),
        name="gossip",
    )(w, factors_rx.reshape(2, 8, 1024), factors_ry.reshape(2, 8, 1024))
    rows = 512 // CHUNKS
    mixed, next_rx, next_ry = pl.pallas_call(
        mix,
        out_shape=(
            jax.ShapeDtypeStruct((2, 256, 1024), F32),
            jax.ShapeDtypeStruct((2, 8, 1024), F32),
            jax.ShapeDtypeStruct((2, 8, 1024), F32),
        ),
        in_specs=[anyspec, vmem, vmem],
        out_specs=(anyspec, anyspec, anyspec),
        scratch_shapes=[
            vm((CHUNKS, rows, 1024), F32),
            vm((CHUNKS, rows, 1024), F32),
            dma((CHUNKS,)),
            dma((CHUNKS,)),
            dma((4,)),
        ],
        compiler_params=pltpu.CompilerParams(vmem_limit_bytes=24 * 1024 * 1024),
        name="mix",
    )(w, h, r)
    return (
        mixed.reshape(1, 1, 2, 256, 1024),
        next_rx.reshape(1, 1, 2, 8, 1024),
        next_ry.reshape(1, 1, 2, 8, 1024),
    )


def solution(mesh):
    wide = P("rx", "ry", None, "tp", None)
    narrow = P("rx", "ry", None, None, None)
    return jax.shard_map(
        per_device, mesh=mesh, in_specs=(wide, narrow, narrow), out_specs=(wide, narrow, narrow), check_vma=False
    )
```

time: 142 us -> 50.8 us (0.36)
  the two profiles are of different devices: /device:TPU:1 before, /device:TPU:6 now
where the time goes in v1:
time: 50.8 us; the launch traced here: 50.6 us
  Pallas kernels  46.7 us (92%)
  local copies, waits for them, and re-layouts  3.26 us (6%)
  between operations  0.65 us (1%)
    pallas_call x1, Pallas kernels, per_device(): pl.pallas_call(gossip, out_shape=(jax.ShapeDtypeStruct((2, 4, 8, 1024), F...  44.6 us
    unnamed x6, local copies, waits for them, and re-layouts  3.26 us
    pallas_call x1, Pallas kernels, per_device(): pl.pallas_call(mix, out_shape=(jax.ShapeDtypeStruct((2, 256, 1024), F32),...  2.07 us

profile of v1, /device:TPU:6, one launch (start us, length us, event | category | flops | bytes accessed | tf_op | source)
XLA Modules:
  0.0 50.6 jit_solution(14369544084861177788)
XLA Ops:
  0.6 0.0 copy-start
  0.6 1.6 %copy-done = f32[1,1,2,256,1024]{4,3,2,1,0:T(8,128)S(1)} copy-done((f32[1,1,2,256,1024]{4,3,2,1,0:T(8,128)S(1)}, f32[1,1,2,256,1024]{4,3,2,1,0:T(8,128)}, u32[]{:S(2)}) %copy-start) | copy-done | bytes 2097176
  2.2 0.0 copy-start.1
  2.2 0.8 %copy-done.1 = f32[1,1,2,8,1024]{4,3,2,1,0:T(8,128)S(1)} copy-done((f32[1,1,2,8,1024]{4,3,2,1,0:T(8,128)S(1)}, f32[1,1,2,8,1024]{4,3,2,1,0:T(8,128)}, u32[]{:S(2)}) %copy-start.1) | copy-done | bytes 65560
  3.1 0.0 copy-start.2
  3.1 0.8 %copy-done.2 = f32[1,1,2,8,1024]{4,3,2,1,0:T(8,128)S(1)} copy-done((f32[1,1,2,8,1024]{4,3,2,1,0:T(8,128)S(1)}, f32[1,1,2,8,1024]{4,3,2,1,0:T(8,128)}, u32[]{:S(2)}) %copy-start.2) | copy-done | bytes 65560
  3.9 44.6 %gossip.1 = (f32[2,4,8,1024]{3,2,1,0:T(8,128)S(1)}, f32[2,4,8,256]{3,2,1,0:T(8,128)S(1)}) custom-call(f32[2,256,1024]{2,1,0:T(8,128)S(1)} %bitcast.6, f32[2,8,1024]{2,1,0:T(8,128)S(1)} %bitcast.8, f32[2,8,1024]{2,1,0:T(8,128)S(1)} %bitcast.9), custom_call_target="tpu_custom_call" | custom-call | tf_op jit(solution)/shard_map/gossip/pallas_call | solution.py:367
  48.5 2.1 %mix.1 = (f32[2,256,1024]{2,1,0:T(8,128)}, f32[2,8,1024]{2,1,0:T(8,128)}, f32[2,8,1024]{2,1,0:T(8,128)}) custom-call(f32[2,256,1024]{2,1,0:T(8,128)S(1)} %bitcast.7, f32[2,4,8,256]{3,2,1,0:T(8,128)S(1)} %get-tuple-element.8.h_ref, f32[2,4,8,1024]{3,2,1,0:T(8,128)S(1)} %get-tuple-element.9.r_ref), custom_call_target="tpu_custom_call" | custom-call | tf_op jit(solution)/shard_map/mix/pallas_call | solution.py:420
Async XLA Ops:
  0.6 1.6 %copy-start = (f32[1,1,2,256,1024]{4,3,2,1,0:T(8,128)S(1)}, f32[1,1,2,256,1024]{4,3,2,1,0:T(8,128)}, u32[]{:S(2)}) copy-start(f32[1,1,2,256,1024]{4,3,2,1,0:T(8,128)} %param.3) | copy-start | bytes 6291460
  2.2 0.8 %copy-start.1 = (f32[1,1,2,8,1024]{4,3,2,1,0:T(8,128)S(1)}, f32[1,1,2,8,1024]{4,3,2,1,0:T(8,128)}, u32[]{:S(2)}) copy-start(f32[1,1,2,8,1024]{4,3,2,1,0:T(8,128)} %param.4) | copy-start | bytes 196612
  3.1 0.8 %copy-start.2 = (f32[1,1,2,8,1024]{4,3,2,1,0:T(8,128)S(1)}, f32[1,1,2,8,1024]{4,3,2,1,0:T(8,128)}, u32[]{:S(2)}) copy-start(f32[1,1,2,8,1024]{4,3,2,1,0:T(8,128)} %param.5) | copy-start | bytes 196612

commit v2 on v0

v2 whole, which is shorter than its diff:
```python
import jax
import jax.numpy as jnp
from jax import lax
from jax.experimental import pallas as pl
from jax.experimental.pallas import tpu as pltpu
from jax.sharding import PartitionSpec as P

MESH = pl.DeviceIdType.MESH
F32 = jnp.float32
BF16 = jnp.bfloat16
NZ, NY = 8, 4
Z_ORDER = (4, 3, 5, 2, 6, 1, 7, 0)
NT = (((1,), (1,)), ((), ()))
NN = (((1,), (0,)), ((), ()))


def split3(x):
    hi = x.astype(BF16)
    rest = x - hi.astype(F32)
    mid = rest.astype(BF16)
    low = (rest - mid.astype(F32)).astype(BF16)
    return hi, mid, low


def dot6(x, wh, wm, wl, dims):
    rows = x.shape[0]
    hi, mid, low = split3(x)
    a = lax.dot_general(jnp.concatenate([hi, mid, low], 0), wh, dims, preferred_element_type=F32)
    b = lax.dot_general(jnp.concatenate([hi, mid], 0), wm, dims, preferred_element_type=F32)
    c = lax.dot_general(hi, wl, dims, preferred_element_type=F32)
    small = (c + b[rows:]) + a[2 * rows :]
    return a[:rows] + ((a[rows : 2 * rows] + b[:rows]) + small)


def gossip(
    w_hbm, fx_hbm, fy_hbm, r_out, h_out,
    q, wv, wh, wm, wl, own, nb, p, c, inbox, g1, g2, f,
    load_sem, fac_s, fac_r, own_s, own_r, sum_s, sum_r, all_s, all_r, g1_s, g1_r, g2_s, g2_r, heard,
):
    a, b, t = lax.axis_index("rx"), lax.axis_index("ry"), lax.axis_index("tp")
    z, y = t // NY, t % NY
    zs = [(z + k) % NZ for k in range(NZ)]
    ys = [(y + k) % NY for k in range(NY)]
    near = [((a + 3) % 4, b), (a, (b + 3) % 4), ((a + 1) % 4, b), (a, (b + 1) % 4)]
    turn = [2 * (a % 2), 2 * (b % 2)]
    owner = [(slot + turn[slot % 2]) % NY for slot in range(4)]
    from_owner = [(y + NY - owner[slot]) % NY for slot in range(4)]
    mine = (y + jnp.where(y % 2 == 0, turn[0], turn[1])) % 4
    step = jnp.where(mine >= 2, 1, 3)
    far_a = jnp.where(y % 2 == 0, (a + step) % 4, a)
    far_b = jnp.where(y % 2 == 0, b, (b + step) % 4)
    my_matrix = jnp.where(mine >= 2, 0, 1)
    my_tile = my_matrix * 32 + mine * NZ + z
    far_tile = my_matrix * 32 + ((mine + 2) % 4) * NZ + z

    def at(zz, yy):
        return (a, b, zz * NY + yy)

    def send(src, dst, ssem, rsem, dev):
        pltpu.make_async_remote_copy(
            src_ref=src, dst_ref=dst, send_sem=ssem, recv_sem=rsem, device_id=dev, device_id_type=MESH
        ).start()

    def counted(ref, sem):
        return pltpu.make_async_remote_copy(
            src_ref=ref, dst_ref=ref, send_sem=sem, recv_sem=sem, device_id=near_dev[0], device_id_type=MESH
        )

    near_dev = [(ra, rb, t) for ra, rb in near]

    loads = []
    for m in range(2):
        loads.append(pltpu.make_async_copy(fx_hbm.at[m], q.at[m, 2], load_sem.at[m]))
        loads.append(pltpu.make_async_copy(fy_hbm.at[m], q.at[m, 3], load_sem.at[2 + m]))
    for m in range(2):
        loads.append(pltpu.make_async_copy(w_hbm.at[m], wv.at[m], load_sem.at[4 + m]))
    for load in loads:
        load.start()

    beside = [at(zs[1], y), at(zs[7], y)]
    across = [at(z, ys[1]), at(z, ys[3])]
    barrier = pltpu.get_barrier_semaphore()
    for dev in near_dev + beside + across:
        pl.semaphore_signal(barrier, inc=1, device_id=dev, device_id_type=MESH)
    rounds = [beside + across, beside + across, beside, [at(zs[2], y), at(zs[6], y)], beside]

    def tell(i):
        for dev in rounds[i]:
            pl.semaphore_signal(heard.at[i], inc=1, device_id=dev, device_id_type=MESH)

    def hear(i):
        pl.semaphore_wait(heard.at[i], len(rounds[i]))

    pl.semaphore_wait(barrier, 8)
    tell(0)
    for m in range(2):
        for s in (2, 3):
            loads[2 * m + s - 2].wait()
            send(q.at[m, s], q.at[m, s - 2], fac_s, fac_r.at[m], near_dev[s])

    def project(first, m):
        x = q[m, pl.ds(first, 2)].reshape(16, 1024)
        res = dot6(x, wh[m], wm[m], wl[m], NT)
        for i in range(2):
            own[m, first + i] = res[8 * i : 8 * i + 8]
        for s in (first, first + 1):
            send(own.at[m, s], nb.at[m, s ^ 2], own_s, own_r.at[1 - first // 2, m], near_dev[s])

    for m in range(2):
        loads[4 + m].wait()
        hi, mid, low = split3(wv[m])
        wh[m], wm[m], wl[m] = hi, mid, low
    hear(0)
    tell(1)
    for m in range(2):
        project(2, m)
    hear(1)
    tell(2)
    for m in range(2):
        counted(q.at[m, pl.ds(0, 2)], fac_r.at[m]).wait_recv()
        project(0, m)
        if m == 0:
            hear(2)
            tell(3)
    hear(3)
    tell(4)

    def differ(first, m):
        part = pl.ds(first, 2)
        counted(nb.at[m, part], own_r.at[first // 2, m]).wait_recv()
        p[m, part] = own[m, part] - nb[m, part]

    def back(first, m):
        x = p[m, pl.ds(first, 2)].reshape(16, 256)
        res = dot6(x, wh[m], wm[m], wl[m], NN)
        for i in range(2):
            for j in range(NZ):
                c[m * 32 + (first + i) * NZ + j] = res[8 * i : 8 * i + 8, 128 * j : 128 * j + 128]

    def share(first, m):
        here = m == (0 if first == 2 else 1)
        for k in Z_ORDER:
            for s in (first, first + 1):
                src = c.at[m * 32 + s * NZ + zs[k]]
                slot = ((NZ - k) % NZ) * NY + from_owner[s] + (0 if here else 32)
                ra, rb = (a, b) if here else near[s]
                dev = (ra, rb, zs[k] * NY + owner[s])
                if here and k == 0:

                    @pl.when(owner[s] != y)
                    def _():
                        send(src, inbox.at[slot], sum_s, sum_r, dev)
                else:
                    send(src, inbox.at[slot], sum_s, sum_r, dev)

    for m in range(2):
        differ(0, m)
        back(0, m)
    hear(4)
    for m in range(2):
        share(0, m)
    for m in range(2):
        differ(2, m)
        back(2, m)
        share(2, m)

    rows = p[...].reshape(64, 256)
    gram = lax.dot_general(
        rows, jnp.concatenate([rows, rows], 0), NT, precision=lax.Precision.HIGHEST, preferred_element_type=F32
    )
    lane = lax.broadcasted_iota(jnp.int32, (8, 128), 1)
    block = (lane // 8) % 8
    tile = jnp.zeros((8, 128), F32)
    for i in range(8):
        tile = tile + jnp.where(block == i, gram[8 * i : 8 * i + 8], 0.0)
    g1[y] = tile
    for k in (2, 1, 3):
        send(g1.at[y], g1.at[y], g1_s, g1_r, at(z, ys[k]))
    counted(g1.at[pl.ds(0, NY - 1)], g1_r).wait_recv()
    g2[z] = (g1[0] + g1[1]) + (g1[2] + g1[3])
    for k in Z_ORDER[:-1]:
        send(g2.at[z], g2.at[z], g2_s, g2_r, at(zs[k], y))

    counted(inbox.at[pl.ds(1, 63)], sum_r).wait_recv()
    parts = [c[my_tile], inbox[1], inbox[2], inbox[3]]
    for i in range(4, 64):
        parts[i % 4] = parts[i % 4] + inbox[i]
    f[my_tile] = (parts[0] + parts[1]) + (parts[2] + parts[3])
    ordered = [(k, j) for k in range(NZ) for j in range(NY)]
    ordered.sort(key=lambda kj: -(min(kj[0], NZ - kj[0]) + 2 * min(kj[1], NY - kj[1])))
    for k, j in ordered:
        there = zs[k] * NY + ys[j]
        send(f.at[my_tile], f.at[far_tile], all_s, all_r, (far_a, far_b, there))
        if k or j:
            send(f.at[my_tile], f.at[my_tile], all_s, all_r, (a, b, there))

    counted(g2.at[pl.ds(0, NZ - 1)], g2_r).wait_recv()
    tile = ((g2[0] + g2[1]) + (g2[2] + g2[3])) + ((g2[4] + g2[5]) + (g2[6] + g2[7]))
    row = lax.broadcasted_iota(jnp.int32, (8, 128), 0)
    cols = [tile] + [pltpu.roll(tile, 128 - j, 1) for j in range(1, 8)]
    lower, inverse_diag = [], []
    for k in range(8):
        pivot = jnp.broadcast_to(cols[k][k : k + 1], (8, 128))
        inv = 1.0 / jnp.sqrt(pivot)
        col = cols[k] * inv
        lower.append(jnp.where(row > k, col, 0.0))
        inverse_diag.append(inv)
        for j in range(k + 1, 8):
            cols[j] = cols[j] - col * jnp.broadcast_to(col[j : j + 1], (8, 128))
    inv_cols = [jnp.where(row == j, 1.0, 0.0).astype(F32) for j in range(8)]
    for k in range(8):
        for j in range(k + 1):
            cur = inv_cols[j]
            pivot_row = jnp.broadcast_to(cur[k : k + 1], (8, 128)) * inverse_diag[k]
            cur = cur - lower[k] * pivot_row
            inv_cols[j] = jnp.where(row == k, pivot_row, cur)

    def solve(i, x):
        total = inv_cols[0][:, 8 * i : 8 * i + 1] * x[0:1]
        for j in range(1, 8):
            total = total + inv_cols[j][:, 8 * i : 8 * i + 1] * x[j : j + 1]
        return total

    for m in range(2):
        for s in range(4):
            h_out[m, s] = solve(4 * m + s, p[m, s])

    counted(f.at[pl.ds(0, 63)], all_r).wait_recv()
    for m in range(2):
        for s in range(4):
            r_out[m, s] = solve(4 * m + s, jnp.concatenate([f[m * 32 + s * NZ + j] for j in range(NZ)], 1))

    counted(q.at[pl.ds(0, 2), pl.ds(2, 2)], fac_s).wait_send()
    counted(own, own_s).wait_send()
    counted(c.at[pl.ds(0, 63)], sum_s).wait_send()
    counted(f.at[pl.ds(0, 63)], all_s).wait_send()
    counted(g1.at[pl.ds(0, NY - 1)], g1_s).wait_send()
    counted(g2.at[pl.ds(0, NZ - 1)], g2_s).wait_send()


CHUNKS = 4


def mix(w_ref, h_ref, r_ref, out_hbm, nx_hbm, ny_hbm, ov, out_sem, small_sem):
    rows = 512 // CHUNKS
    stores = []
    for m in range(2):
        stores.append(pltpu.make_async_copy(r_ref.at[m, 2], nx_hbm.at[m], small_sem.at[m]))
        stores.append(pltpu.make_async_copy(r_ref.at[m, 3], ny_hbm.at[m], small_sem.at[2 + m]))
    for store in stores:
        store.start()
    for m in range(2):
        h = h_ref[m].reshape(32, 256)
        r = r_ref[m].reshape(32, 1024)
        hh, hl, _ = split3(h)
        rh, rl, _ = split3(r)
        left = jnp.concatenate([hh, hh, hl], 0)
        right = jnp.concatenate([rh, rl, rh], 0)
        for i in range(m * CHUNKS // 2, (m + 1) * CHUNKS // 2):
            start = (i * rows) % 256
            term = lax.dot_general(
                left[:, start : start + rows], right, (((0,), (0,)), ((), ())), preferred_element_type=F32
            )
            ov[i] = w_ref[m, start : start + rows] - 0.2 * term
            store = pltpu.make_async_copy(ov.at[i], out_hbm.at[m, pl.ds(start, rows)], out_sem.at[i])
            store.start()
            stores.append(store)
    for store in stores:
        store.wait()


def per_device(weights, factors_rx, factors_ry):
    w = weights.reshape(2, 256, 1024)
    vm = pltpu.VMEM
    dma = pltpu.SemaphoreType.DMA
    anyspec = pl.BlockSpec(memory_space=pl.ANY)
    hbm = pl.BlockSpec(memory_space=pltpu.HBM)
    vmem = pl.BlockSpec(memory_space=pltpu.VMEM)
    tile = (8, 128)
    r, h = pl.pallas_call(
        gossip,
        out_shape=(
            jax.ShapeDtypeStruct((2, 4, 8, 1024), F32),
            jax.ShapeDtypeStruct((2, 4, 8, 256), F32),
        ),
        in_specs=[hbm] * 3,
        out_specs=(vmem, vmem),
        scratch_shapes=[
            vm((2, 4, 8, 1024), F32),
            vm((2, 256, 1024), F32),
            vm((2, 256, 1024), BF16),
            vm((2, 256, 1024), BF16),
            vm((2, 256, 1024), BF16),
            vm((2, 4, 8, 256), F32),
            vm((2, 4, 8, 256), F32),
            vm((2, 4, 8, 256), F32),
            vm((64, *tile), F32),
            vm((64, *tile), F32),
            vm((NY, *tile), F32),
            vm((NZ, *tile), F32),
            vm((64, *tile), F32),
            dma((6,)),
            dma, dma((2,)),
            dma, dma((2, 2)),
            dma, dma,
            dma, dma,
            dma, dma,
            dma, dma,
            pltpu.SemaphoreType.REGULAR((5,)),
        ],
        compiler_params=pltpu.CompilerParams(
            collective_id=0, has_side_effects=True, vmem_limit_bytes=24 * 1024 * 1024
        ),
        name="gossip",
    )(*[pltpu.with_memory_space_constraint(x, pltpu.HBM) for x in (w, factors_rx.reshape(2, 8, 1024), factors_ry.reshape(2, 8, 1024))])
    rows = 512 // CHUNKS
    mixed, next_rx, next_ry = pl.pallas_call(
        mix,
        out_shape=(
            jax.ShapeDtypeStruct((2, 256, 1024), F32),
            jax.ShapeDtypeStruct((2, 8, 1024), F32),
            jax.ShapeDtypeStruct((2, 8, 1024), F32),
        ),
        in_specs=[vmem, vmem, vmem],
        out_specs=(anyspec, anyspec, anyspec),
        scratch_shapes=[
            vm((CHUNKS, rows, 1024), F32),
            dma((CHUNKS,)),
            dma((4,)),
        ],
        compiler_params=pltpu.CompilerParams(vmem_limit_bytes=24 * 1024 * 1024),
        name="mix",
    )(w, h, r)
    return (
        mixed.reshape(1, 1, 2, 256, 1024),
        next_rx.reshape(1, 1, 2, 8, 1024),
        next_ry.reshape(1, 1, 2, 8, 1024),
    )


def solution(mesh):
    wide = P("rx", "ry", None, "tp", None)
    narrow = P("rx", "ry", None, None, None)
    return jax.shard_map(
        per_device, mesh=mesh, in_specs=(wide, narrow, narrow), out_specs=(wide, narrow, narrow), check_vma=False
    )
```

time: 142 us -> 44.4 us (0.31)
  starting transfers between devices: 52.2 us -> 0 us
  Pallas kernels: 0 us -> 43.5 us
  blocking collectives: 32 us -> 0 us
  waiting for transfers between devices: 19.5 us -> 0 us
  other arithmetic: 14.7 us -> 0 us
  local copies, waits for them, and re-layouts: 12.9 us -> 0.01 us
  matrix products: 8.68 us -> 0 us
    pallas_call x0 -> x2, Pallas kernels: none -> 43.5 us  [the longest x1 41.9 us: per_device(): pl.pallas_call(gossip, out_shape=(jax.ShapeDtypeStruct((2, 4, 8, 1024), F...]
    ppermute x10 -> x0, starting transfers between devices: 39.6 us -> none  [the longest x4 17.2 us: extended(): lax.ppermute(leading, axis, [(b, a) for a, b in up])]
    all_to_all x2 -> x0, blocking collectives: 32 us -> none  [the longest x1 17.3 us: sent_to_all(): lax.all_to_all(jnp.broadcast_to(x[None], (size, *x.shape)), axis, 0, 0, t...]
    all_to_all x1 -> x0, starting transfers between devices: 12.6 us -> none  [sent_to_all(): lax.all_to_all(jnp.broadcast_to(x[None], (size, *x.shape)), axis, 0, 0, t...]
    another operation x7 -> x0, other arithmetic: 11.2 us -> none  [the longest x4 6.07 us: per_device(): lower_factor = jnp.linalg.cholesky(gram_total)]
    all_to_all x1 -> x0, waiting for transfers between devices: 11.1 us -> none  [sent_to_all(): lax.all_to_all(jnp.broadcast_to(x[None], (size, *x.shape)), axis, 0, 0, t...]
    ppermute x10 -> x0, waiting for transfers between devices: 8.44 us -> none  [the longest x4 5.13 us: extended(): lax.ppermute(leading, axis, [(b, a) for a, b in up])]
    dot_general x4 -> x0, matrix products: 8.38 us -> none  [the longest x1 3.66 us: per_device(): jnp.einsum('emrk,mdk->emrd', factor_set, local_rows, precision=highest)]
  transfers between devices with their start and end apart: 11 -> 0, of which waited for: 5 -> 0; matrix products, arithmetic and copies ran while one was open for 0% -> 0% of each run, Pallas kernels for 0% -> 0%
where the time goes in v2:
time: 44.4 us; the launch traced here: 44.2 us
  Pallas kernels  43.5 us (98%)
  between operations  0.65 us (1%)
    pallas_call x1, Pallas kernels, per_device(): pl.pallas_call(gossip, out_shape=(jax.ShapeDtypeStruct((2, 4, 8, 1024), F...  41.9 us
    pallas_call x1, Pallas kernels, per_device(): pl.pallas_call(mix, out_shape=(jax.ShapeDtypeStruct((2, 256, 1024), F32),...  1.68 us

profile of v2, /device:TPU:1, one launch (start us, length us, event | category | flops | bytes accessed | tf_op | source)
XLA Modules:
  0.0 44.2 jit_solution(15676173033596544522)
XLA Ops:
  0.6 0.0 copy-start
  0.6 41.9 %gossip.1 = (f32[2,4,8,1024]{3,2,1,0:T(8,128)S(1)}, f32[2,4,8,256]{3,2,1,0:T(8,128)S(1)}) custom-call(f32[2,256,1024]{2,1,0:T(8,128)} %bitcast.6, f32[2,8,1024]{2,1,0:T(8,128)} %bitcast.8, f32[2,8,1024]{2,1,0:T(8,128)} %bitcast.9), custom_call_target="tpu_custom_call" | custom-call | tf_op jit(solution)/shard_map/gossip/pallas_call | solution.py:280
  42.5 0.0 copy-done
  42.5 1.7 %mix.1 = (f32[2,256,1024]{2,1,0:T(8,128)}, f32[2,8,1024]{2,1,0:T(8,128)}, f32[2,8,1024]{2,1,0:T(8,128)}) custom-call(f32[2,256,1024]{2,1,0:T(8,128)S(1)} %bitcast.7, f32[2,4,8,256]{3,2,1,0:T(8,128)S(1)} %get-tuple-element.8.h_ref, f32[2,4,8,1024]{3,2,1,0:T(8,128)S(1)} %get-tuple-element.9.r_ref), custom_call_target="tpu_custom_call" | custom-call | tf_op jit(solution)/shard_map/mix/pallas_call | solution.py:317
Async XLA Ops:
  0.6 41.9 %copy-start = (f32[1,1,2,256,1024]{4,3,2,1,0:T(8,128)S(1)}, f32[1,1,2,256,1024]{4,3,2,1,0:T(8,128)}, u32[]{:S(2)}) copy-start(f32[1,1,2,256,1024]{4,3,2,1,0:T(8,128)} %param.3) | copy-start | bytes 6291460

commit v3 on v2

--- a/solution.py
+++ b/solution.py
@@ -9,7 +9,7 @@
 F32 = jnp.float32
 BF16 = jnp.bfloat16
 NZ, NY = 8, 4
-Z_ORDER = (4, 3, 5, 2, 6, 1, 7, 0)
+Z_ORDER = (4, 5, 3, 6, 2, 7, 1, 0)
 NT = (((1,), (1,)), ((), ()))
 NN = (((1,), (0,)), ((), ()))
 
@@ -32,57 +32,37 @@
     return a[:rows] + ((a[rows : 2 * rows] + b[:rows]) + small)
 
 
+def spread():
+    far_first = lambda kj: -(min(kj[0], NZ - kj[0]) + min(kj[1], NY - kj[1]))
+    sides = [
+        sorted([(k, j) for k in side for j in range(NY)], key=far_first)
+        for side in (range(1, 5), range(5, NZ), range(1))
+    ]
+    order = [((i + 0.5) / len(side), n, kj) for n, side in enumerate(sides) for i, kj in enumerate(side)]
+    return [kj for _, _, kj in sorted(order)]
+
+
 def gossip(
     w_hbm, fx_hbm, fy_hbm, r_out, h_out,
     q, wv, wh, wm, wl, own, nb, p, c, inbox, g1, g2, f,
     load_sem, fac_s, fac_r, own_s, own_r, sum_s, sum_r, all_s, all_r, g1_s, g1_r, g2_s, g2_r, heard,
 ):
     a, b, t = lax.axis_index("rx"), lax.axis_index("ry"), lax.axis_index("tp")
-    z, y = t // NY, t % NY
-    zs = [(z + k) % NZ for k in range(NZ)]
-    ys = [(y + k) % NY for k in range(NY)]
-    near = [((a + 3) % 4, b), (a, (b + 3) % 4), ((a + 1) % 4, b), (a, (b + 1) % 4)]
-    turn = [2 * (a % 2), 2 * (b % 2)]
-    owner = [(slot + turn[slot % 2]) % NY for slot in range(4)]
-    from_owner = [(y + NY - owner[slot]) % NY for slot in range(4)]
-    mine = (y + jnp.where(y % 2 == 0, turn[0], turn[1])) % 4
-    step = jnp.where(mine >= 2, 1, 3)
-    far_a = jnp.where(y % 2 == 0, (a + step) % 4, a)
-    far_b = jnp.where(y % 2 == 0, b, (b + step) % 4)
-    my_matrix = jnp.where(mine >= 2, 0, 1)
-    my_tile = my_matrix * 32 + mine * NZ + z
-    far_tile = my_matrix * 32 + ((mine + 2) % 4) * NZ + z
+    z, y = lax.div(t, NY), lax.rem(t, NY)
+    zs = [lax.rem(z + k, NZ) for k in range(NZ)]
+    ys = [lax.rem(y + k, NY) for k in range(NY)]
+    near = [(lax.rem(a + 3, 4), b), (a, lax.rem(b + 3, 4)), (lax.rem(a + 1, 4), b), (a, lax.rem(b + 1, 4))]
+    near_dev = [(ra, rb, t) for ra, rb in near]
 
     def at(zz, yy):
         return (a, b, zz * NY + yy)
-
-    def send(src, dst, ssem, rsem, dev):
-        pltpu.make_async_remote_copy(
-            src_ref=src, dst_ref=dst, send_sem=ssem, recv_sem=rsem, device_id=dev, device_id_type=MESH
-        ).start()
-
-    def counted(ref, sem):
-        return pltpu.make_async_remote_copy(
-            src_ref=ref, dst_ref=ref, send_sem=sem, recv_sem=sem, device_id=near_dev[0], device_id_type=MESH
-        )
-
-    near_dev = [(ra, rb, t) for ra, rb in near]
-
-    loads = []
-    for m in range(2):
-        loads.append(pltpu.make_async_copy(fx_hbm.at[m], q.at[m, 2], load_sem.at[m]))
-        loads.append(pltpu.make_async_copy(fy_hbm.at[m], q.at[m, 3], load_sem.at[2 + m]))
-    for m in range(2):
-        loads.append(pltpu.make_async_copy(w_hbm.at[m], wv.at[m], load_sem.at[4 + m]))
-    for load in loads:
-        load.start()
 
     beside = [at(zs[1], y), at(zs[7], y)]
     across = [at(z, ys[1]), at(z, ys[3])]
     barrier = pltpu.get_barrier_semaphore()
     for dev in near_dev + beside + across:
         pl.semaphore_signal(barrier, inc=1, device_id=dev, device_id_type=MESH)
-    rounds = [beside + across, beside + across, beside, [at(zs[2], y), at(zs[6], y)], beside]
+    rounds = [across + beside, across + [at(zs[2], y), at(zs[6], y)], [at(zs[k], y) for k in Z_ORDER[:-1]]]
 
     def tell(i):
         for dev in rounds[i]:
@@ -91,78 +71,101 @@
     def hear(i):
         pl.semaphore_wait(heard.at[i], len(rounds[i]))
 
+    def send(src, dst, ssem, rsem, dev):
+        pltpu.make_async_remote_copy(
+            src_ref=src, dst_ref=dst, send_sem=ssem, recv_sem=rsem, device_id=dev, device_id_type=MESH
+        ).start()
+
+    def counted(ref, sem):
+        return pltpu.make_async_remote_copy(
+            src_ref=ref, dst_ref=ref, send_sem=sem, recv_sem=sem, device_id=near_dev[0], device_id_type=MESH
+        )
+
+    loads = [
+        pltpu.make_async_copy(fx_hbm, q.at[2], load_sem.at[0]),
+        pltpu.make_async_copy(fy_hbm, q.at[3], load_sem.at[1]),
+        pltpu.make_async_copy(w_hbm.at[0], wv.at[0], load_sem.at[2]),
+        pltpu.make_async_copy(w_hbm.at[1], wv.at[1], load_sem.at[3]),
+    ]
+    for load in loads:
+        load.start()
+
+    turn = [2 * lax.rem(a, 2), 2 * lax.rem(a + b, 2)]
+    owner = [lax.rem(slot + turn[slot % 2], NY) for slot in range(4)]
+    from_owner = [lax.rem(y + NY - owner[slot], NY) for slot in range(4)]
+    odd = lax.rem(y, 2)
+    mine = lax.rem(y + (1 - odd) * turn[0] + odd * turn[1], NY)
+    step = 3 - 2 * lax.div(mine, 2)
+    far_a, far_b = lax.rem(a + (1 - odd) * step, 4), lax.rem(b + odd * step, 4)
+    my_matrix = 1 - lax.div(mine, 2)
+    my_tile = (mine * NZ + z) * 2 + my_matrix
+    far_tile = (lax.rem(mine + 2, 4) * NZ + z) * 2 + my_matrix
+
     pl.semaphore_wait(barrier, 8)
     tell(0)
-    for m in range(2):
-        for s in (2, 3):
-            loads[2 * m + s - 2].wait()
-            send(q.at[m, s], q.at[m, s - 2], fac_s, fac_r.at[m], near_dev[s])
-
-    def project(first, m):
-        x = q[m, pl.ds(first, 2)].reshape(16, 1024)
-        res = dot6(x, wh[m], wm[m], wl[m], NT)
-        for i in range(2):
-            own[m, first + i] = res[8 * i : 8 * i + 8]
+    for s in (2, 3):
+        loads[s - 2].wait()
+        send(q.at[s], q.at[s - 2], fac_s, fac_r, near_dev[s])
+
+    def project(first):
+        for m in range(2):
+            x = q[pl.ds(first, 2), m].reshape(16, 1024)
+            res = dot6(x, wh[m], wm[m], wl[m], NT)
+            for i in range(2):
+                own[first + i, m] = res[8 * i : 8 * i + 8]
         for s in (first, first + 1):
-            send(own.at[m, s], nb.at[m, s ^ 2], own_s, own_r.at[1 - first // 2, m], near_dev[s])
-
-    for m in range(2):
-        loads[4 + m].wait()
-        hi, mid, low = split3(wv[m])
-        wh[m], wm[m], wl[m] = hi, mid, low
-    hear(0)
-    tell(1)
-    for m in range(2):
-        project(2, m)
-    hear(1)
-    tell(2)
-    for m in range(2):
-        counted(q.at[m, pl.ds(0, 2)], fac_r.at[m]).wait_recv()
-        project(0, m)
-        if m == 0:
-            hear(2)
-            tell(3)
-    hear(3)
-    tell(4)
-
-    def differ(first, m):
+            send(own.at[s], nb.at[s ^ 2], own_s, own_r.at[1 - first // 2], near_dev[s])
+
+    def differ(first):
         part = pl.ds(first, 2)
-        counted(nb.at[m, part], own_r.at[first // 2, m]).wait_recv()
-        p[m, part] = own[m, part] - nb[m, part]
+        counted(nb.at[part], own_r.at[first // 2]).wait_recv()
+        p[part] = own[part] - nb[part]
 
     def back(first, m):
-        x = p[m, pl.ds(first, 2)].reshape(16, 256)
+        x = p[pl.ds(first, 2), m].reshape(16, 256)
         res = dot6(x, wh[m], wm[m], wl[m], NN)
         for i in range(2):
             for j in range(NZ):
-                c[m * 32 + (first + i) * NZ + j] = res[8 * i : 8 * i + 8, 128 * j : 128 * j + 128]
-
-    def share(first, m):
-        here = m == (0 if first == 2 else 1)
-        for k in Z_ORDER:
+                c[((first + i) * NZ + j) * 2 + m] = res[8 * i : 8 * i + 8, 128 * j : 128 * j + 128]
+
+    def share(first, m, order):
+        here = m == 1 - first // 2
+        for k in order:
             for s in (first, first + 1):
-                src = c.at[m * 32 + s * NZ + zs[k]]
-                slot = ((NZ - k) % NZ) * NY + from_owner[s] + (0 if here else 32)
+                src = c.at[(s * NZ + zs[k]) * 2 + m]
+                dst = inbox.at[((NZ - k) % NZ) * NY + from_owner[s] + (0 if here else 32)]
                 ra, rb = (a, b) if here else near[s]
                 dev = (ra, rb, zs[k] * NY + owner[s])
                 if here and k == 0:
 
                     @pl.when(owner[s] != y)
                     def _():
-                        send(src, inbox.at[slot], sum_s, sum_r, dev)
+                        send(src, dst, sum_s, sum_r, dev)
                 else:
-                    send(src, inbox.at[slot], sum_s, sum_r, dev)
-
-    for m in range(2):
-        differ(0, m)
+                    send(src, dst, sum_s, sum_r, dev)
+
+    for m in range(2):
+        loads[2 + m].wait()
+        hi, mid, low = split3(wv[m])
+        wh[m], wm[m], wl[m] = hi, mid, low
+    project(2)
+    hear(0)
+    tell(1)
+    counted(q.at[pl.ds(0, 2)], fac_r).wait_recv()
+    hear(1)
+    tell(2)
+    project(0)
+    differ(0)
+    for m in range(2):
         back(0, m)
-    hear(4)
-    for m in range(2):
-        share(0, m)
-    for m in range(2):
-        differ(2, m)
-        back(2, m)
-        share(2, m)
+    hear(2)
+    share(0, 0, Z_ORDER)
+    share(0, 1, Z_ORDER[:3])
+    differ(2)
+    back(2, 0)
+    share(2, 0, Z_ORDER)
+    back(2, 1)
+    share(2, 1, Z_ORDER[:3])
 
     rows = p[...].reshape(64, 256)
     gram = lax.dot_general(
@@ -176,6 +179,9 @@
     g1[y] = tile
     for k in (2, 1, 3):
         send(g1.at[y], g1.at[y], g1_s, g1_r, at(z, ys[k]))
+    for k in Z_ORDER[3:]:
+        share(0, 1, (k,))
+        share(2, 1, (k,))
     counted(g1.at[pl.ds(0, NY - 1)], g1_r).wait_recv()
     g2[z] = (g1[0] + g1[1]) + (g1[2] + g1[3])
     for k in Z_ORDER[:-1]:
@@ -186,9 +192,7 @@
     for i in range(4, 64):
         parts[i % 4] = parts[i % 4] + inbox[i]
     f[my_tile] = (parts[0] + parts[1]) + (parts[2] + parts[3])
-    ordered = [(k, j) for k in range(NZ) for j in range(NY)]
-    ordered.sort(key=lambda kj: -(min(kj[0], NZ - kj[0]) + 2 * min(kj[1], NY - kj[1])))
-    for k, j in ordered:
+    for k, j in spread():
         there = zs[k] * NY + ys[j]
         send(f.at[my_tile], f.at[far_tile], all_s, all_r, (far_a, far_b, there))
         if k or j:
@@ -223,14 +227,14 @@
 
     for m in range(2):
         for s in range(4):
-            h_out[m, s] = solve(4 * m + s, p[m, s])
+            h_out[m, s] = solve(2 * s + m, p[s, m])
 
     counted(f.at[pl.ds(0, 63)], all_r).wait_recv()
     for m in range(2):
         for s in range(4):
-            r_out[m, s] = solve(4 * m + s, jnp.concatenate([f[m * 32 + s * NZ + j] for j in range(NZ)], 1))
-
-    counted(q.at[pl.ds(0, 2), pl.ds(2, 2)], fac_s).wait_send()
+            r_out[m, s] = solve(2 * s + m, jnp.concatenate([f[(s * NZ + j) * 2 + m] for j in range(NZ)], 1))
+
+    counted(q.at[pl.ds(2, 2)], fac_s).wait_send()
     counted(own, own_s).wait_send()
     counted(c.at[pl.ds(0, 63)], sum_s).wait_send()
     counted(f.at[pl.ds(0, 63)], all_s).wait_send()
@@ -238,7 +242,7 @@
     counted(g2.at[pl.ds(0, NZ - 1)], g2_s).wait_send()
 
 
-CHUNKS = 4
+CHUNKS = 8
 
 
 def mix(w_ref, h_ref, r_ref, out_hbm, nx_hbm, ny_hbm, ov, out_sem, small_sem):
@@ -286,27 +290,27 @@
         in_specs=[hbm] * 3,
         out_specs=(vmem, vmem),
         scratch_shapes=[
-            vm((2, 4, 8, 1024), F32),
+            vm((4, 2, 8, 1024), F32),
             vm((2, 256, 1024), F32),
             vm((2, 256, 1024), BF16),
             vm((2, 256, 1024), BF16),
             vm((2, 256, 1024), BF16),
-            vm((2, 4, 8, 256), F32),
-            vm((2, 4, 8, 256), F32),
-            vm((2, 4, 8, 256), F32),
+            vm((4, 2, 8, 256), F32),
+            vm((4, 2, 8, 256), F32),
+            vm((4, 2, 8, 256), F32),
             vm((64, *tile), F32),
             vm((64, *tile), F32),
             vm((NY, *tile), F32),
             vm((NZ, *tile), F32),
             vm((64, *tile), F32),
-            dma((6,)),
+            dma((4,)),
+            dma, dma,
             dma, dma((2,)),
-            dma, dma((2, 2)),
-            dma, dma,
-            dma, dma,
-            dma, dma,
-            dma, dma,
-            pltpu.SemaphoreType.REGULAR((5,)),
+            dma, dma,
+            dma, dma,
+            dma, dma,
+            dma, dma,
+            pltpu.SemaphoreType.REGULAR((3,)),
         ],
         compiler_params=pltpu.CompilerParams(
             collective_id=0, has_side_effects=True, vmem_limit_bytes=24 * 1024 * 1024

time: 44.4 us -> 43.4 us (0.977)
  Pallas kernels: 43.5 us -> 42.7 us
    pallas_call x1, Pallas kernels: 41.9 us -> 41 us  [per_device(): pl.pallas_call(gossip, out_shape=(jax.ShapeDtypeStruct((2, 4, 8, 1024), F...]
where the time goes in v3:
time: 43.4 us; the launch traced here: 43.3 us
  Pallas kernels  42.7 us (98%)
  between operations  0.65 us (1%)
    pallas_call x1, Pallas kernels, per_device(): pl.pallas_call(gossip, out_shape=(jax.ShapeDtypeStruct((2, 4, 8, 1024), F...  41 us
    pallas_call x1, Pallas kernels, per_device(): pl.pallas_call(mix, out_shape=(jax.ShapeDtypeStruct((2, 256, 1024), F32),...  1.7 us

profile of v3, /device:TPU:1, one launch (start us, length us, event | category | flops | bytes accessed | tf_op | source)
XLA Modules:
  0.0 43.3 jit_solution(14544833546572550849)
XLA Ops:
  0.6 0.0 copy-start
  0.6 41.0 %gossip.1 = (f32[2,4,8,1024]{3,2,1,0:T(8,128)S(1)}, f32[2,4,8,256]{3,2,1,0:T(8,128)S(1)}) custom-call(f32[2,256,1024]{2,1,0:T(8,128)} %bitcast.6, f32[2,8,1024]{2,1,0:T(8,128)} %bitcast.8, f32[2,8,1024]{2,1,0:T(8,128)} %bitcast.9), custom_call_target="tpu_custom_call" | custom-call | tf_op jit(solution)/shard_map/gossip/pallas_call | solution.py:284
  41.6 0.0 copy-done
  41.6 1.7 %mix.1 = (f32[2,256,1024]{2,1,0:T(8,128)}, f32[2,8,1024]{2,1,0:T(8,128)}, f32[2,8,1024]{2,1,0:T(8,128)}) custom-call(f32[2,256,1024]{2,1,0:T(8,128)S(1)} %bitcast.7, f32[2,4,8,256]{3,2,1,0:T(8,128)S(1)} %get-tuple-element.8.h_ref, f32[2,4,8,1024]{3,2,1,0:T(8,128)S(1)} %get-tuple-element.9.r_ref), custom_call_target="tpu_custom_call" | custom-call | tf_op jit(solution)/shard_map/mix/pallas_call | solution.py:321
Async XLA Ops:
  0.6 41.0 %copy-start = (f32[1,1,2,256,1024]{4,3,2,1,0:T(8,128)S(1)}, f32[1,1,2,256,1024]{4,3,2,1,0:T(8,128)}, u32[]{:S(2)}) copy-start(f32[1,1,2,256,1024]{4,3,2,1,0:T(8,128)} %param.3) | copy-start | bytes 6291460

commit v4 on v3

--- a/solution.py
+++ b/solution.py
@@ -32,20 +32,13 @@
     return a[:rows] + ((a[rows : 2 * rows] + b[:rows]) + small)
 
 
-def spread():
-    far_first = lambda kj: -(min(kj[0], NZ - kj[0]) + min(kj[1], NY - kj[1]))
-    sides = [
-        sorted([(k, j) for k in side for j in range(NY)], key=far_first)
-        for side in (range(1, 5), range(5, NZ), range(1))
-    ]
-    order = [((i + 0.5) / len(side), n, kj) for n, side in enumerate(sides) for i, kj in enumerate(side)]
-    return [kj for _, _, kj in sorted(order)]
+GATHER_ORDER = [(zz, yy) for zz in range(NZ) for yy in range(NY)]
 
 
 def gossip(
     w_hbm, fx_hbm, fy_hbm, r_out, h_out,
-    q, wv, wh, wm, wl, own, nb, p, c, inbox, g1, g2, f,
-    load_sem, fac_s, fac_r, own_s, own_r, sum_s, sum_r, all_s, all_r, g1_s, g1_r, g2_s, g2_r, heard,
+    q, wv, wh, wm, wl, own, nb, p, c, inbox, g1, g2, g3, f,
+    load_sem, fac_s, fac_r, own_s, own_r, sum_s, sum_r, all_s, all_r, g1_s, g1_r, g2_s, g2_r, g3_s, g3_r, heard,
 ):
     a, b, t = lax.axis_index("rx"), lax.axis_index("ry"), lax.axis_index("tp")
     z, y = lax.div(t, NY), lax.rem(t, NY)
@@ -156,50 +149,64 @@
     tell(2)
     project(0)
     differ(0)
-    for m in range(2):
-        back(0, m)
-    hear(2)
-    share(0, 0, Z_ORDER)
-    share(0, 1, Z_ORDER[:3])
-    differ(2)
-    back(2, 0)
-    share(2, 0, Z_ORDER)
-    back(2, 1)
-    share(2, 1, Z_ORDER[:3])
-
-    rows = p[...].reshape(64, 256)
+
+    rows = p[0:2].reshape(32, 256)
     gram = lax.dot_general(
-        rows, jnp.concatenate([rows, rows], 0), NT, precision=lax.Precision.HIGHEST, preferred_element_type=F32
+        rows, jnp.concatenate([rows] * 4, 0), NT, precision=lax.Precision.HIGHEST, preferred_element_type=F32
     )
     lane = lax.broadcasted_iota(jnp.int32, (8, 128), 1)
-    block = (lane // 8) % 8
+    block = (lane // 8) % 4
     tile = jnp.zeros((8, 128), F32)
-    for i in range(8):
+    for i in range(4):
         tile = tile + jnp.where(block == i, gram[8 * i : 8 * i + 8], 0.0)
     g1[y] = tile
     for k in (2, 1, 3):
         send(g1.at[y], g1.at[y], g1_s, g1_r, at(z, ys[k]))
-    for k in Z_ORDER[3:]:
-        share(0, 1, (k,))
-        share(2, 1, (k,))
+    for m in range(2):
+        back(0, m)
+    hear(2)
+    for k in Z_ORDER[:4]:
+        for m in range(2):
+            share(0, m, (k,))
+    differ(2)
+    for m in range(2):
+        back(2, m)
+    for k in Z_ORDER[:4]:
+        for m in range(2):
+            share(2, m, (k,))
+    for k in Z_ORDER[4:6]:
+        for m in range(2):
+            share(0, m, (k,))
+            share(2, m, (k,))
+
     counted(g1.at[pl.ds(0, NY - 1)], g1_r).wait_recv()
     g2[z] = (g1[0] + g1[1]) + (g1[2] + g1[3])
     for k in Z_ORDER[:-1]:
         send(g2.at[z], g2.at[z], g2_s, g2_r, at(zs[k], y))
+    for k in Z_ORDER[6:]:
+        for m in range(2):
+            share(0, m, (k,))
+            share(2, m, (k,))
+    counted(g2.at[pl.ds(0, NZ - 1)], g2_r).wait_recv()
+    g3[2] = ((g2[0] + g2[1]) + (g2[2] + g2[3])) + ((g2[4] + g2[5]) + (g2[6] + g2[7]))
+    for s in (0, 1):
+        send(g3.at[2], g3.at[s], g3_s, g3_r, near_dev[s])
 
     counted(inbox.at[pl.ds(1, 63)], sum_r).wait_recv()
     parts = [c[my_tile], inbox[1], inbox[2], inbox[3]]
     for i in range(4, 64):
         parts[i % 4] = parts[i % 4] + inbox[i]
     f[my_tile] = (parts[0] + parts[1]) + (parts[2] + parts[3])
-    for k, j in spread():
-        there = zs[k] * NY + ys[j]
+    for zz, yy in GATHER_ORDER:
+        there = zz * NY + yy
         send(f.at[my_tile], f.at[far_tile], all_s, all_r, (far_a, far_b, there))
-        if k or j:
+
+        @pl.when(t != there)
+        def _():
             send(f.at[my_tile], f.at[my_tile], all_s, all_r, (a, b, there))
 
-    counted(g2.at[pl.ds(0, NZ - 1)], g2_r).wait_recv()
-    tile = ((g2[0] + g2[1]) + (g2[2] + g2[3])) + ((g2[4] + g2[5]) + (g2[6] + g2[7]))
+    counted(g3.at[pl.ds(0, 2)], g3_r).wait_recv()
+    tile = jnp.where(lane < 32, g3[2], jnp.where(lane < 48, g3[0], g3[1]))
     row = lax.broadcasted_iota(jnp.int32, (8, 128), 0)
     cols = [tile] + [pltpu.roll(tile, 128 - j, 1) for j in range(1, 8)]
     lower, inverse_diag = [], []
@@ -240,13 +247,13 @@
     counted(f.at[pl.ds(0, 63)], all_s).wait_send()
     counted(g1.at[pl.ds(0, NY - 1)], g1_s).wait_send()
     counted(g2.at[pl.ds(0, NZ - 1)], g2_s).wait_send()
-
-
-CHUNKS = 8
+    counted(g3.at[pl.ds(0, 2)], g3_s).wait_send()
+
+
+COLUMNS = 256
 
 
 def mix(w_ref, h_ref, r_ref, out_hbm, nx_hbm, ny_hbm, ov, out_sem, small_sem):
-    rows = 512 // CHUNKS
     stores = []
     for m in range(2):
         stores.append(pltpu.make_async_copy(r_ref.at[m, 2], nx_hbm.at[m], small_sem.at[m]))
@@ -254,19 +261,16 @@
     for store in stores:
         store.start()
     for m in range(2):
-        h = h_ref[m].reshape(32, 256)
-        r = r_ref[m].reshape(32, 1024)
-        hh, hl, _ = split3(h)
-        rh, rl, _ = split3(r)
+        hh, hl, _ = split3(h_ref[m].reshape(32, 256))
         left = jnp.concatenate([hh, hh, hl], 0)
-        right = jnp.concatenate([rh, rl, rh], 0)
-        for i in range(m * CHUNKS // 2, (m + 1) * CHUNKS // 2):
-            start = (i * rows) % 256
-            term = lax.dot_general(
-                left[:, start : start + rows], right, (((0,), (0,)), ((), ())), preferred_element_type=F32
-            )
-            ov[i] = w_ref[m, start : start + rows] - 0.2 * term
-            store = pltpu.make_async_copy(ov.at[i], out_hbm.at[m, pl.ds(start, rows)], out_sem.at[i])
+        for i in range(1024 // COLUMNS):
+            part = pl.ds(i * COLUMNS, COLUMNS)
+            rh, rl, _ = split3(r_ref[m, :, :, part].reshape(32, COLUMNS))
+            right = jnp.concatenate([rh, rl, rh], 0)
+            term = lax.dot_general(left, right, (((0,), (0,)), ((), ())), preferred_element_type=F32)
+            n = m * (1024 // COLUMNS) + i
+            ov[n] = w_ref[m, :, part] - 0.2 * term
+            store = pltpu.make_async_copy(ov.at[n], out_hbm.at[m, :, part], out_sem.at[n])
             store.start()
             stores.append(store)
     for store in stores:
@@ -302,10 +306,12 @@
             vm((64, *tile), F32),
             vm((NY, *tile), F32),
             vm((NZ, *tile), F32),
+            vm((3, *tile), F32),
             vm((64, *tile), F32),
             dma((4,)),
             dma, dma,
             dma, dma((2,)),
+            dma, dma,
             dma, dma,
             dma, dma,
             dma, dma,
@@ -317,7 +323,6 @@
         ),
         name="gossip",
     )(*[pltpu.with_memory_space_constraint(x, pltpu.HBM) for x in (w, factors_rx.reshape(2, 8, 1024), factors_ry.reshape(2, 8, 1024))])
-    rows = 512 // CHUNKS
     mixed, next_rx, next_ry = pl.pallas_call(
         mix,
         out_shape=(
@@ -328,8 +333,8 @@
         in_specs=[vmem, vmem, vmem],
         out_specs=(anyspec, anyspec, anyspec),
         scratch_shapes=[
-            vm((CHUNKS, rows, 1024), F32),
-            dma((CHUNKS,)),
+            vm((2048 // COLUMNS, 256, COLUMNS), F32),
+            dma((2048 // COLUMNS,)),
             dma((4,)),
         ],
         compiler_params=pltpu.CompilerParams(vmem_limit_bytes=24 * 1024 * 1024),

time: 43.4 us -> 42.2 us (0.972)
  Pallas kernels: 42.7 us -> 41.4 us
    pallas_call x1, Pallas kernels: 41 us -> 39.7 us  [per_device(): pl.pallas_call(gossip, out_shape=(jax.ShapeDtypeStruct((2, 4, 8, 1024), F...]
where the time goes in v4:
time: 42.2 us; the launch traced here: 42.1 us
  Pallas kernels  41.4 us (98%)
  between operations  0.65 us (2%)
    pallas_call x1, Pallas kernels, per_device(): pl.pallas_call(gossip, out_shape=(jax.ShapeDtypeStruct((2, 4, 8, 1024), F...  39.7 us
    pallas_call x1, Pallas kernels, per_device(): pl.pallas_call(mix, out_shape=(jax.ShapeDtypeStruct((2, 256, 1024), F32),...  1.7 us

profile of v4, /device:TPU:1, one launch (start us, length us, event | category | flops | bytes accessed | tf_op | source)
XLA Modules:
  0.0 42.1 jit_solution(12674226306698007296)
XLA Ops:
  0.6 0.0 copy-start
  0.6 39.7 %gossip.1 = (f32[2,4,8,1024]{3,2,1,0:T(8,128)S(1)}, f32[2,4,8,256]{3,2,1,0:T(8,128)S(1)}) custom-call(f32[2,256,1024]{2,1,0:T(8,128)} %bitcast.6, f32[2,8,1024]{2,1,0:T(8,128)} %bitcast.8, f32[2,8,1024]{2,1,0:T(8,128)} %bitcast.9), custom_call_target="tpu_custom_call" | custom-call | tf_op jit(solution)/shard_map/gossip/pallas_call | solution.py:288
  40.4 0.0 copy-done
  40.4 1.7 %mix.1 = (f32[2,256,1024]{2,1,0:T(8,128)}, f32[2,8,1024]{2,1,0:T(8,128)}, f32[2,8,1024]{2,1,0:T(8,128)}) custom-call(f32[2,256,1024]{2,1,0:T(8,128)S(1)} %bitcast.7, f32[2,4,8,256]{3,2,1,0:T(8,128)S(1)} %get-tuple-element.8.h_ref, f32[2,4,8,1024]{3,2,1,0:T(8,128)S(1)} %get-tuple-element.9.r_ref), custom_call_target="tpu_custom_call" | custom-call | tf_op jit(solution)/shard_map/mix/pallas_call | solution.py:326
Async XLA Ops:
  0.6 39.7 %copy-start = (f32[1,1,2,256,1024]{4,3,2,1,0:T(8,128)S(1)}, f32[1,1,2,256,1024]{4,3,2,1,0:T(8,128)}, u32[]{:S(2)}) copy-start(f32[1,1,2,256,1024]{4,3,2,1,0:T(8,128)} %param.3) | copy-start | bytes 6291460

commit v5 on v4

--- a/solution.py
+++ b/solution.py
@@ -37,7 +37,7 @@
 
 def gossip(
     w_hbm, fx_hbm, fy_hbm, r_out, h_out,
-    q, wv, wh, wm, wl, own, nb, p, c, inbox, g1, g2, g3, f,
+    q, wv, wh, wm, wl, th, tm, tl, own, nb, p, c, inbox, g1, g2, g3, f,
     load_sem, fac_s, fac_r, own_s, own_r, sum_s, sum_r, all_s, all_r, g1_s, g1_r, g2_s, g2_r, g3_s, g3_r, heard,
 ):
     a, b, t = lax.axis_index("rx"), lax.axis_index("ry"), lax.axis_index("tp")
@@ -103,7 +103,10 @@
     def project(first):
         for m in range(2):
             x = q[pl.ds(first, 2), m].reshape(16, 1024)
-            res = dot6(x, wh[m], wm[m], wl[m], NT)
+            if first == 2:
+                res = dot6(x, wh[m], wm[m], wl[m], NT)
+            else:
+                res = dot6(x, th[m], tm[m], tl[m], NN)
             for i in range(2):
                 own[first + i, m] = res[8 * i : 8 * i + 8]
         for s in (first, first + 1):
@@ -144,9 +147,11 @@
     project(2)
     hear(0)
     tell(1)
-    counted(q.at[pl.ds(0, 2)], fac_r).wait_recv()
+    for m in range(2):
+        th[m], tm[m], tl[m] = wh[m].T, wm[m].T, wl[m].T
     hear(1)
     tell(2)
+    counted(q.at[pl.ds(0, 2)], fac_r).wait_recv()
     project(0)
     differ(0)
 
@@ -299,6 +304,9 @@
             vm((2, 256, 1024), BF16),
             vm((2, 256, 1024), BF16),
             vm((2, 256, 1024), BF16),
+            vm((2, 1024, 256), BF16),
+            vm((2, 1024, 256), BF16),
+            vm((2, 1024, 256), BF16),
             vm((4, 2, 8, 256), F32),
             vm((4, 2, 8, 256), F32),
             vm((4, 2, 8, 256), F32),

time: 42.2 us -> 41.6 us (0.986)
  Pallas kernels: 41.4 us -> 40.8 us
    pallas_call x1, Pallas kernels: 39.7 us -> 39.1 us  [per_device(): pl.pallas_call(gossip, out_shape=(jax.ShapeDtypeStruct((2, 4, 8, 1024), F...]
where the time goes in v5:
time: 41.6 us; the launch traced here: 41.5 us
  Pallas kernels  40.8 us (98%)
  between operations  0.65 us (2%)
    pallas_call x1, Pallas kernels, per_device(): pl.pallas_call(gossip, out_shape=(jax.ShapeDtypeStruct((2, 4, 8, 1024), F...  39.1 us
    pallas_call x1, Pallas kernels, per_device(): pl.pallas_call(mix, out_shape=(jax.ShapeDtypeStruct((2, 256, 1024), F32),...  1.71 us

profile of v5, /device:TPU:1, one launch (start us, length us, event | category | flops | bytes accessed | tf_op | source)
XLA Modules:
  0.0 41.5 jit_solution(1604547131165491751)
XLA Ops:
  0.6 0.0 copy-start
  0.6 39.1 %gossip.1 = (f32[2,4,8,1024]{3,2,1,0:T(8,128)S(1)}, f32[2,4,8,256]{3,2,1,0:T(8,128)S(1)}) custom-call(f32[2,256,1024]{2,1,0:T(8,128)} %bitcast.6, f32[2,8,1024]{2,1,0:T(8,128)} %bitcast.8, f32[2,8,1024]{2,1,0:T(8,128)} %bitcast.9), custom_call_target="tpu_custom_call" | custom-call | tf_op jit(solution)/shard_map/gossip/pallas_call | solution.py:293
  39.8 0.0 copy-done
  39.8 1.7 %mix.1 = (f32[2,256,1024]{2,1,0:T(8,128)}, f32[2,8,1024]{2,1,0:T(8,128)}, f32[2,8,1024]{2,1,0:T(8,128)}) custom-call(f32[2,256,1024]{2,1,0:T(8,128)S(1)} %bitcast.7, f32[2,4,8,256]{3,2,1,0:T(8,128)S(1)} %get-tuple-element.8.h_ref, f32[2,4,8,1024]{3,2,1,0:T(8,128)S(1)} %get-tuple-element.9.r_ref), custom_call_target="tpu_custom_call" | custom-call | tf_op jit(solution)/shard_map/mix/pallas_call | solution.py:334
Async XLA Ops:
  0.6 39.1 %copy-start = (f32[1,1,2,256,1024]{4,3,2,1,0:T(8,128)S(1)}, f32[1,1,2,256,1024]{4,3,2,1,0:T(8,128)}, u32[]{:S(2)}) copy-start(f32[1,1,2,256,1024]{4,3,2,1,0:T(8,128)} %param.3) | copy-start | bytes 6291460

commit v6 on v5

--- a/solution.py
+++ b/solution.py
@@ -32,7 +32,7 @@
     return a[:rows] + ((a[rows : 2 * rows] + b[:rows]) + small)
 
 
-GATHER_ORDER = [(zz, yy) for zz in range(NZ) for yy in range(NY)]
+GATHER_ORDER = [(zz, j) for zz in range(NZ) for j in (2, 1, 3, 0)]
 
 
 def gossip(
@@ -202,13 +202,16 @@
     for i in range(4, 64):
         parts[i % 4] = parts[i % 4] + inbox[i]
     f[my_tile] = (parts[0] + parts[1]) + (parts[2] + parts[3])
-    for zz, yy in GATHER_ORDER:
-        there = zz * NY + yy
+    for zz, j in GATHER_ORDER:
+        there = zz * NY + ys[j]
         send(f.at[my_tile], f.at[far_tile], all_s, all_r, (far_a, far_b, there))
-
-        @pl.when(t != there)
-        def _():
+        if j:
             send(f.at[my_tile], f.at[my_tile], all_s, all_r, (a, b, there))
+        else:
+
+            @pl.when(z != zz)
+            def _():
+                send(f.at[my_tile], f.at[my_tile], all_s, all_r, (a, b, there))
 
     counted(g3.at[pl.ds(0, 2)], g3_r).wait_recv()
     tile = jnp.where(lane < 32, g3[2], jnp.where(lane < 48, g3[0], g3[1]))

time: 41.6 us -> 41.9 us (level)
  no operation moved by 1% of the time
where the time goes in v6:
time: 41.9 us; the launch traced here: 41.6 us
  Pallas kernels  40.9 us (98%)
  between operations  0.65 us (2%)
    pallas_call x1, Pallas kernels, per_device(): pl.pallas_call(gossip, out_shape=(jax.ShapeDtypeStruct((2, 4, 8, 1024), F...  39.2 us
    pallas_call x1, Pallas kernels, per_device(): pl.pallas_call(mix, out_shape=(jax.ShapeDtypeStruct((2, 256, 1024), F32),...  1.7 us

profile of v6, /device:TPU:1, one launch (start us, length us, event | category | flops | bytes accessed | tf_op | source)
XLA Modules:
  0.0 41.6 jit_solution(11115048940021706082)
XLA Ops:
  0.6 0.0 copy-start
  0.6 39.2 %gossip.1 = (f32[2,4,8,1024]{3,2,1,0:T(8,128)S(1)}, f32[2,4,8,256]{3,2,1,0:T(8,128)S(1)}) custom-call(f32[2,256,1024]{2,1,0:T(8,128)} %bitcast.6, f32[2,8,1024]{2,1,0:T(8,128)} %bitcast.8, f32[2,8,1024]{2,1,0:T(8,128)} %bitcast.9), custom_call_target="tpu_custom_call" | custom-call | tf_op jit(solution)/shard_map/gossip/pallas_call | solution.py:296
  39.9 0.0 copy-done
  39.9 1.7 %mix.1 = (f32[2,256,1024]{2,1,0:T(8,128)}, f32[2,8,1024]{2,1,0:T(8,128)}, f32[2,8,1024]{2,1,0:T(8,128)}) custom-call(f32[2,256,1024]{2,1,0:T(8,128)S(1)} %bitcast.7, f32[2,4,8,256]{3,2,1,0:T(8,128)S(1)} %get-tuple-element.8.h_ref, f32[2,4,8,1024]{3,2,1,0:T(8,128)S(1)} %get-tuple-element.9.r_ref), custom_call_target="tpu_custom_call" | custom-call | tf_op jit(solution)/shard_map/mix/pallas_call | solution.py:337
Async XLA Ops:
  0.6 39.3 %copy-start = (f32[1,1,2,256,1024]{4,3,2,1,0:T(8,128)S(1)}, f32[1,1,2,256,1024]{4,3,2,1,0:T(8,128)}, u32[]{:S(2)}) copy-start(f32[1,1,2,256,1024]{4,3,2,1,0:T(8,128)} %param.3) | copy-start | bytes 6291460
